TPU v7x, 32 devices: a whole 2x2x4 slice. The times are simulated.
32 devices in a mesh: ep: 8 (over y, x, core), dp: 4 (over z).
Axes of the slice: x: 2, y: 2, z: 4, core: 2. Of those that a mesh axis runs over, the one named last changes fastest.
Arguments:
- resid: bfloat16 [512, 4096], P(('ep', 'dp')), may hold values from -6 to 6
- queries: bfloat16 [512, 8192], P(('ep', 'dp')), may hold values from -4.5 to 4.5
- new_keys: bfloat16 [512, 512], P(('ep', 'dp')), may hold values from -4.5 to 4.5
- new_values: bfloat16 [512, 512], P(('ep', 'dp')), may hold values from -6 to 6
- cache_keys: bfloat16 [512, 128, 512], P(('ep', 'dp')), may hold values from -4.5 to 4.5
- cache_values: bfloat16 [512, 128, 512], P(('ep', 'dp')), may hold values from -6 to 6
- cache_len: int32 [512], P(('ep', 'dp')), may hold values from 1 to 128
- out_proj: bfloat16 [8192, 4096], P('ep'), may hold values from -0.0625 to 0.0625
- norm_gain: float32 [4096], replicated, may hold values from 0.1 to 1.9
- router: bfloat16 [4096, 16], replicated, may hold values from -4 to 4
- expert_ids: int32 [512, 8], P(('ep', 'dp')), may hold values from 0 to 15, all different within a row; in each aligned block of 16 rows (0 to 15, 16 to 31, ...) at most 14 rows name the same one
- gate_slab: bfloat16 [32, 4096, 384], P(('ep', 'dp')), may hold values from -0.09375 to 0.09375
- up_slab: bfloat16 [32, 4096, 384], P(('ep', 'dp')), may hold values from -0.09375 to 0.09375
- down_slab: bfloat16 [32, 384, 4096], P(('ep', 'dp')), may hold values from -0.21875 to 0.21875
Outputs:
- mixed: float32 [512, 4096], P(('ep', 'dp'))
Inputs may be any that keep to these rules, and one draw needn't show every extreme that they name: `expert_ids`: each row names 8 different experts; among the rows of one device no expert is named by more than 14 rows.
All inputs are finite; a program needn't handle non-finite values.
Results may differ from a plain program's by a relative error of at most 0.009.
Values may be sent and summed in bfloat16 or wider, within the bound.
A program may use at most 128 MiB of HBM per device.

v0:
```python
import math

import jax
import jax.numpy as jnp
from jax import lax
from jax.experimental import pallas as pl
from jax.experimental.pallas import tpu as pltpu
from jax.sharding import PartitionSpec as P

D = 4096
H = 64
KVH = 4
HD = 128
TOP = 8


def attend(queries, new_keys, new_values, cache_keys, cache_values, cache_len):
    local_rows = queries.shape[0]
    cache_span = cache_keys.shape[1]
    group_size = H // KVH
    query_heads = queries.reshape(local_rows, KVH, group_size, HD)
    past_keys = cache_keys.reshape(local_rows, cache_span, KVH, HD)
    past_values = cache_values.reshape(local_rows, cache_span, KVH, HD)
    score_scale = 1.0 / math.sqrt(HD)
    past_scores = (
        jnp.einsum("tgqd,tcgd->tgqc", query_heads, past_keys, preferred_element_type=jnp.float32)
        * score_scale
    )
    own_scores = (
        jnp.einsum(
            "tgqd,tgd->tgq",
            query_heads,
            new_keys.reshape(local_rows, KVH, HD),
            preferred_element_type=jnp.float32,
        )
        * score_scale
    )
    is_valid = lax.broadcasted_iota(jnp.int32, (local_rows, cache_span), 1) < cache_len[:, None]
    past_scores = jnp.where(is_valid[:, None, None, :], past_scores, -1e30)
    peak_score = jnp.maximum(jnp.max(past_scores, axis=3), own_scores)
    past_exp = jnp.exp(past_scores - peak_score[..., None])
    own_exp = jnp.exp(own_scores - peak_score)
    denom_sum = jnp.sum(past_exp, axis=3) + own_exp
    past_weights = (past_exp / denom_sum[..., None]).astype(jnp.bfloat16)
    own_weights = (own_exp / denom_sum).astype(jnp.bfloat16)
    blended = jnp.einsum(
        "tgqc,tcgd->tgqd", past_weights, past_values, preferred_element_type=jnp.float32
    )
    blended = blended + own_weights.astype(jnp.float32)[..., None] * new_values.reshape(
        local_rows, KVH, 1, HD
    ).astype(jnp.float32)
    return blended.reshape(local_rows, H * HD).astype(jnp.bfloat16)


MESH = pl.DeviceIdType.MESH
VMEM_LIMIT = 66_000_000


class Place:
    def __init__(self, side, depth):
        self.side, self.depth = side, depth
        ep = lax.axis_index("ep")
        self.ep = ep
        self.core = lax.rem(ep, 2)
        self.x = lax.rem(ep // 2, side)
        self.y = ep // (2 * side)
        self.z = lax.axis_index("dp")

    def at(self, dy=0, dx=0, dz=0, flip=False):
        y, x = self.line(dy, dx)
        z = lax.rem(self.z + dz, self.depth) if dz else self.z
        core = 1 - self.core if flip else self.core
        return ((y * self.side + x) * 2 + core, z)

    def line(self, dy, dx):
        return lax.rem(self.y + dy, self.side), lax.rem(self.x + dx, self.side)


def greet(devices):
    barrier = pltpu.get_barrier_semaphore()
    for device in devices:
        pl.semaphore_signal(barrier, inc=1, device_id=device, device_id_type=MESH)
    pl.semaphore_wait(barrier, len(devices))


def remote(src, dst, send, recv, device):
    return pltpu.make_async_remote_copy(
        src_ref=src, dst_ref=dst, send_sem=send, recv_sem=recv, device_id=device, device_id_type=MESH
    )


def slices_of(width, extra=0):
    step = 512
    cuts = [[start, step] for start in range(0, width, step)]
    cuts[-1][1] += extra
    return cuts


def reduce_shapes(side, depth, rows, width):
    n = width // 512
    lines = side * side
    bf, dma = jnp.bfloat16, pltpu.SemaphoreType.DMA
    tall = depth * rows
    return [
        pltpu.VMEM((side, side, tall, width), bf),
        pltpu.VMEM((side - 1, side, tall, width), bf),
        pltpu.VMEM((side, tall, width), bf),
        pltpu.VMEM((side - 1, tall, width), bf),
        pltpu.VMEM((depth, rows, width), bf),
        pltpu.VMEM((max(depth - 1, 1), rows, width), bf),
        dma((n, 2)),
        dma((n, side, side, 2)),
        dma((n, side, 2)),
        dma((n, depth, 2)),
    ]


def reduce_scatter(here, rows, width, produce, finish, lags, part, scratch):
    in1, in2, sum2, in3, sum3, in4, sem1, sem2, sem3, sem4 = scratch
    side, depth = here.side, here.depth
    cuts = slices_of(width)
    sends = []

    def core_copy(s):
        start, size = cuts[s]
        cols = pl.ds(start, size)
        return remote(
            part.at[:, :, 1 - here.core, :, cols],
            in1.at[:, :, :, cols],
            sem1.at[s, 0],
            sem1.at[s, 1],
            here.at(flip=True),
        )

    def offsets(s, a, b):
        return (a, b) if s % 2 == 0 else (b, a)

    def first_copy(s, ja, kb, sending):
        cols = pl.ds(*cuts[s])
        slot = side - ja - 1
        y, x = here.line(*offsets(s, ja, kb))
        return remote(
            in1.at[y, x, :, cols],
            in2.at[slot, kb, :, cols],
            sem2.at[s, ja, kb, 0],
            sem2.at[s, side - ja if sending else ja, kb, 1],
            here.at(*offsets(s, ja, 0)),
        )

    def second_copy(s, kb, sending):
        cols = pl.ds(*cuts[s])
        return remote(
            sum2.at[kb, :, cols],
            in3.at[side - kb - 1, :, cols],
            sem3.at[s, kb, 0],
            sem3.at[s, side - kb if sending else kb, 1],
            here.at(*offsets(s, 0, kb)),
        )

    def depth_copy(s, jz, sending):
        cols = pl.ds(*cuts[s])
        return remote(
            sum3.at[lax.rem(here.z + jz, depth), :, cols],
            in4.at[depth - jz - 1, :, cols],
            sem4.at[s, jz, 0],
            sem4.at[s, depth - jz if sending else jz, 1],
            here.at(0, 0, jz),
        )

    def go(copy):
        copy.start()
        sends.append(copy)

    def wide(value):
        return value.astype(jnp.float32)

    def phase0(s):
        cols = pl.ds(*cuts[s])
        value = produce(s, cols)
        part[:, :, :, :, cols] = value.astype(jnp.bfloat16).reshape(
            side, side, 2, depth * rows, cuts[s][1]
        )
        go(core_copy(s))

    def phase1(s):
        cols = pl.ds(*cuts[s])
        core_copy(s).wait_recv()
        for a in list(range(1, side)) + [0]:
            for b in list(range(1, side)) + [0]:
                y, x = here.line(*offsets(s, a, b))
                total = wide(part[y, x, here.core, :, cols]) + wide(in1[y, x, :, cols])
                in1[y, x, :, cols] = total.astype(jnp.bfloat16)
                if a:
                    go(first_copy(s, a, b, True))

    def phase2(s):
        cols = pl.ds(*cuts[s])
        for b in list(range(1, side)) + [0]:
            y, x = here.line(*offsets(s, 0, b))
            total = wide(in1[y, x, :, cols])
            for a in range(1, side):
                first_copy(s, a, b, False).wait_recv()
                total = total + wide(in2[a - 1, b, :, cols])
            sum2[b, :, cols] = total.astype(jnp.bfloat16)
            if b:
                go(second_copy(s, b, True))

    def phase3(s):
        cols = pl.ds(*cuts[s])
        total = wide(sum2[0, :, cols])
        for b in range(1, side):
            second_copy(s, b, False).wait_recv()
            total = total + wide(in3[b - 1, :, cols])
        if depth == 1:
            finish(s, cols, total)
            return
        sum3[:, :, cols] = total.astype(jnp.bfloat16).reshape(depth, rows, cuts[s][1])
        for jz in range(1, depth):
            go(depth_copy(s, jz, True))

    def phase4(s):
        if depth == 1:
            return
        cols = pl.ds(*cuts[s])
        total = wide(sum3[here.z, :, cols])
        for jz in range(1, depth):
            depth_copy(s, jz, False).wait_recv()
            total = total + wide(in4[jz - 1, :, cols])
        finish(s, cols, total)

    phases = tuple(zip((phase0, phase1, phase2, phase3, phase4), lags))
    for step in range(len(cuts) + phases[-1][1]):
        for phase, lag in phases:
            if 0 <= step - lag < len(cuts):
                phase(step - lag)
    for copy in sends:
        copy.wait_send()


def plane_of(here):
    side = here.side
    return (
        [here.at(flip=True)]
        + [here.at(dy=j) for j in range(1, side)]
        + [here.at(dx=j) for j in range(1, side)]
    )


def projection_kernel(
    side, attended, weight_hbm, resid, gain, router, chosen, hidden, packed, weight, regrouped, part, wsem, ssem, rsem, *scratch
):
    here = Place(side, 1)
    rows = attended.shape[0]
    count = 2 * side * side
    width = attended.shape[1] // count
    z = lax.axis_index("dp")
    load = pltpu.make_async_copy(weight_hbm, weight, wsem)
    load.start()

    def peer(j):
        return lax.rem(here.ep + j, count)

    greet([(peer(j), z) for j in range(1, count)])

    def piece(index):
        return attended.at[:, pl.ds(pl.multiple_of(index * width, 128), width)]

    def exchange(j, sending):
        return remote(
            piece(peer(j)),
            regrouped.at[here.ep],
            ssem.at[j],
            rsem.at[count - j if sending else j],
            (peer(j), z),
        )

    for j in range(1, count):
        exchange(j, True).start()
    regrouped[here.ep] = attended[:, pl.ds(pl.multiple_of(here.ep * width, 128), width)]
    load.wait()
    for j in range(1, count):
        remote(
            piece(peer(j)), regrouped.at[peer(j)], ssem.at[j], rsem.at[j], (peer(j), z)
        ).wait_recv()

    def produce(s, cols):
        left = regrouped[...].reshape(count * rows, width)
        return jnp.dot(left, weight[:, cols], preferred_element_type=jnp.float32)

    def finish(s, cols, total):
        value = resid[:, cols].astype(jnp.float32) + total
        hidden[:, cols] = value
        squares.append(jnp.sum(value * value, axis=1, keepdims=True))

    squares = []

    reduce_scatter(here, rows, hidden.shape[1], produce, finish, (0, 2, 5, 8, 8), part, scratch)
    features = hidden.shape[1]
    scale = lax.rsqrt(jnp.maximum(sum(squares) / features, 0.25))
    logits = jnp.zeros((rows, router.shape[1]), jnp.float32)
    for start, size in slices_of(features):
        cols = pl.ds(start, size)
        normed = (hidden[:, cols] * scale * gain[:, cols]).astype(jnp.bfloat16)
        packed[:, cols] = normed
        logits = logits + jnp.dot(normed, router[cols, :], preferred_element_type=jnp.float32)
    named = chosen[...] > 0
    peak = jnp.max(jnp.where(named, logits, -jnp.inf), axis=1, keepdims=True)
    grown = jnp.where(named, jnp.exp(jnp.where(named, logits - peak, 0.0)), 0.0)
    probs = grown / jnp.sum(grown, axis=1, keepdims=True)
    packed[:, features:] = jnp.zeros((rows, packed.shape[1] - features), jnp.bfloat16)
    packed[:, features : features + router.shape[1]] = probs.astype(jnp.bfloat16)
    for j in range(1, count):
        exchange(j, True).wait_send()


def project(side, attended, out_proj, resid, gain, router, chosen):
    rows, width = resid.shape
    count = 2 * side * side
    dma = pltpu.SemaphoreType.DMA
    vmem = pl.BlockSpec(memory_space=pltpu.VMEM)
    return pl.pallas_call(
        lambda *refs: projection_kernel(side, *refs),
        out_shape=(
            jax.ShapeDtypeStruct((rows, width), jnp.float32),
            jax.ShapeDtypeStruct((rows, width + pl.cdiv(router.shape[1], 128) * 128), jnp.bfloat16),
        ),
        in_specs=[vmem, pl.BlockSpec(memory_space=pl.ANY), vmem, vmem, vmem, vmem],
        out_specs=(vmem, vmem),
        scratch_shapes=[
            pltpu.VMEM(out_proj.shape, jnp.bfloat16),
            pltpu.VMEM((count, rows, attended.shape[1] // count), jnp.bfloat16),
            pltpu.VMEM((side, side, 2, rows, width), jnp.bfloat16),
            dma(()),
            dma((count,)),
            dma((count,)),
        ]
        + reduce_shapes(side, 1, rows, width),
        compiler_params=pltpu.CompilerParams(
            collective_id=0, has_side_effects=True, vmem_limit_bytes=VMEM_LIMIT
        ),
    )(attended, out_proj, resid, gain, router, chosen)


def all_gather(here, own, held, consume, zsem, lsem, csem, send_sem, copy_sem):
    side, depth = here.side, here.depth
    width = D
    cuts = slices_of(width, own.shape[1] - width)
    sends = []
    rows = own.shape[0]

    def rows_of(z):
        return pl.ds(pl.multiple_of(z * rows, rows), rows)

    local_copy = pltpu.make_async_copy(own, held.at[here.y, here.x, here.core, rows_of(here.z)], copy_sem)
    local_copy.start()

    def go(copy):
        copy.start()
        sends.append(copy)

    def depth_copy(s, j, sending):
        cols = pl.ds(*cuts[s])
        z = here.z if sending else lax.rem(here.z + j, depth)
        return remote(
            own.at[:, cols],
            held.at[here.y, here.x, here.core, rows_of(z), cols],
            zsem.at[s, j, 0],
            zsem.at[s, depth - j if sending else j, 1],
            here.at(0, 0, j),
        )

    def line_ref(s, ky, kx, core):
        y, x = here.line(ky, kx)
        return held.at[y, x, core, :, pl.ds(*cuts[s])]

    def plane_send(s, ky, kx, jy, jx):
        ref = line_ref(s, ky, kx, here.core)
        go(
            remote(
                ref,
                ref,
                send_sem.at[s, ky, kx, jy, jx],
                lsem.at[s, (ky - jy) % side, (kx - jx) % side],
                here.at(jy, jx),
            )
        )

    def core_send(s, ky, kx):
        ref = line_ref(s, ky, kx, here.core)
        go(remote(ref, ref, csem.at[s, ky, kx, 0], csem.at[s, ky, kx, 1], here.at(flip=True)))

    def plane_wait(s, ky, kx):
        ref = line_ref(s, ky, kx, here.core)
        remote(ref, ref, send_sem.at[s, 0, 0, 0, 0], lsem.at[s, ky, kx], here.at(flip=True)).wait_recv()

    def core_wait(s, ky, kx):
        ref = line_ref(s, ky, kx, 1 - here.core)
        remote(ref, ref, csem.at[s, ky, kx, 0], csem.at[s, ky, kx, 1], here.at(flip=True)).wait_recv()

    def turn(s, a, b):
        return (a, b) if s % 2 == 0 else (b, a)

    def phase1(s):
        for j in range(1, depth):
            depth_copy(s, j, False).wait_recv()
        for j in range(1, side):
            plane_send(s, 0, 0, *turn(s, j, 0))
            plane_send(s, 0, 0, *turn(s, 0, j))
        core_send(s, 0, 0)

    def phase2(s):
        for k in range(1, side):
            plane_wait(s, *turn(s, k, 0))
            for j in range(1, side):
                plane_send(s, *turn(s, k, 0), *turn(s, 0, j))
            core_send(s, *turn(s, k, 0))

    def phase3(s):
        for b in range(1, side):
            for a in range(side):
                plane_wait(s, *turn(s, a, b))
                core_send(s, *turn(s, a, b))

    def phase0(s):
        for j in range(1, depth):
            go(depth_copy(s, j, True))

    local_copy.wait()
    def phase4(s):
        for a in range(side):
            for b in range(side):
                core_wait(s, a, b)
        consume(s)

    phases = ((phase0, 0), (phase1, 2), (phase2, 4), (phase3, 6), (phase4, 7))
    for step in range(len(cuts) + phases[-1][1]):
        for phase, lag in phases:
            if 0 <= step - lag < len(cuts):
                phase(step - lag)
    for copy in sends:
        copy.wait_send()


def expert_kernel(
    side, depth, own, gate_hbm, up_hbm, down_hbm, mixed,
    gate, up, down, held, act, gate_sum, up_sum, wsem, zsem, lsem, csem, send_sem, copy_sem, *scratch
):
    here = Place(side, depth)
    rows = own.shape[0]
    loads = [
        pltpu.make_async_copy(src.at[0], dst, wsem.at[i])
        for i, (src, dst) in enumerate(((gate_hbm, gate), (up_hbm, up), (down_hbm, down)))
    ]
    for load in loads:
        load.start()
    greet(plane_of(here) + [here.at(0, 0, j) for j in range(1, depth)])
    group = side * 2 * depth * rows

    def rows_at(y):
        return pl.ds(pl.multiple_of(y * group, group), group)

    def consume(s):
        if s == 0:
            loads[0].wait()
            loads[1].wait()
        start = 512 * s

        def step(y, carry):
            block = held[y, :, :, :, start : start + 512].reshape(group, 512)
            for weight, total in ((gate, gate_sum), (up, up_sum)):
                value = jnp.dot(
                    block, weight[start : start + 512, :], preferred_element_type=jnp.float32
                )
                total[rows_at(y), :] = value if s == 0 else total[rows_at(y), :] + value
            return carry

        lax.fori_loop(0, side, step, 0)

    all_gather(here, own, held, consume, zsem, lsem, csem, send_sem, copy_sem)
    loads[2].wait()
    expert = (here.ep * depth + here.z) // 2

    def activate(y, carry):
        tail = held[y, :, :, :, D:].reshape(group, held.shape[-1] - D)
        lane = lax.broadcasted_iota(jnp.int32, tail.shape, 1)
        weight = jnp.sum(
            jnp.where(lane == expert, tail.astype(jnp.float32), 0.0), axis=1, keepdims=True
        )
        gate_val = gate_sum[rows_at(y), :]
        value = gate_val / (1.0 + jnp.exp(-gate_val)) * up_sum[rows_at(y), :] * weight
        act[rows_at(y), :] = value.astype(jnp.bfloat16)
        return carry

    lax.fori_loop(0, side, activate, 0)

    def produce(s, cols):
        return jnp.dot(act[...], down[:, cols], preferred_element_type=jnp.float32)

    def finish(s, cols, total):
        mixed[:, cols] = total

    reduce_scatter(here, rows, mixed.shape[1], produce, finish, (0, 1, 3, 5, 7), held, scratch)


def run_experts(side, depth, packed, gate_slab, up_slab, down_slab):
    rows, width = packed.shape[0], down_slab.shape[2]
    n = width // 512
    dma = pltpu.SemaphoreType.DMA
    count = 2 * side * side * depth
    vmem, anywhere = pl.BlockSpec(memory_space=pltpu.VMEM), pl.BlockSpec(memory_space=pl.ANY)
    return pl.pallas_call(
        lambda *refs: expert_kernel(side, depth, *refs),
        out_shape=jax.ShapeDtypeStruct((rows, width), jnp.float32),
        in_specs=[vmem, anywhere, anywhere, anywhere],
        out_specs=vmem,
        scratch_shapes=[
            pltpu.VMEM(gate_slab.shape[1:], jnp.bfloat16),
            pltpu.VMEM(up_slab.shape[1:], jnp.bfloat16),
            pltpu.VMEM(down_slab.shape[1:], jnp.bfloat16),
            pltpu.VMEM((side, side, 2, depth * rows, packed.shape[1]), jnp.bfloat16),
            pltpu.VMEM((count * rows, gate_slab.shape[2]), jnp.bfloat16),
            pltpu.VMEM((count * rows, gate_slab.shape[2]), jnp.float32),
            pltpu.VMEM((count * rows, gate_slab.shape[2]), jnp.float32),
            dma((3,)),
            dma((n, depth, 2)),
            dma((n, side, side)),
            dma((n, side, side, 2)),
            dma((n, side, side, side, side)),
            dma(()),
        ]
        + reduce_shapes(side, depth, rows, width),
        compiler_params=pltpu.CompilerParams(
            collective_id=1, has_side_effects=True, vmem_limit_bytes=VMEM_LIMIT
        ),
    )(packed, gate_slab, up_slab, down_slab)


def local(
    resid,
    queries,
    new_keys,
    new_values,
    cache_keys,
    cache_values,
    cache_len,
    out_proj,
    norm_gain,
    router,
    expert_ids,
    gate_slab,
    up_slab,
    down_slab,
):
    attended = attend(queries, new_keys, new_values, cache_keys, cache_values, cache_len)
    side = math.isqrt(lax.axis_size("ep") // 2)
    depth = lax.axis_size("dp")
    labels = jnp.arange(router.shape[1], dtype=jnp.int32)
    chosen = jnp.any(expert_ids[:, :, None] == labels[None, None, :], axis=1).astype(jnp.float32)
    hidden, packed = project(
        side, attended, out_proj, resid, norm_gain.reshape(1, -1), router, chosen
    )
    return hidden + run_experts(side, depth, packed, gate_slab, up_slab, down_slab)


def solution(mesh):
    in_specs = (
        P(("ep", "dp"), None),
        P(("ep", "dp"), None),
        P(("ep", "dp"), None),
        P(("ep", "dp"), None),
        P(("ep", "dp"), None, None),
        P(("ep", "dp"), None, None),
        P(("ep", "dp")),
        P("ep", None),
        P(),
        P(),
        P(("ep", "dp"), None),
        P(("ep", "dp"), None, None),
        P(("ep", "dp"), None, None),
        P(("ep", "dp"), None, None),
    )
    out_specs = P(("ep", "dp"), None)
    return jax.shard_map(local, mesh=mesh, in_specs=in_specs, out_specs=out_specs, check_vma=False)
```

profile of v0, /device:TPU:0, one launch (start us, length us, event | category | flops | bytes accessed | tf_op | source)
XLA Modules:
  0.0 101.1 jit_solution(13477078682918430417)
XLA Ops:
  0.0 0.7 iota_compare_fusion.1
  0.7 0.8 copy.21
  1.5 0.1 fusion.21
  1.6 0.6 convert_element_type.35.refs_5_
  2.2 0.7 reshape.55
  2.9 0.7 reshape.51
  3.7 1.0 copy.27
  4.7 0.0 copy-start.2
  4.7 0.2 fusion.25
  4.9 3.0 %fusion.24 = (f32[16,4,16]{2,1,0:T(4,128)S(1)}, f32[16,4,16,128]{3,2,1,0:T(8,128)S(1)}) fusion(bf16[16,4,16,128]{3,2,1,0:T(8,128)(2,1)S(1)} %bitcast.39, pred[16,128]{1,0:T(8,128)(4,1)S(1)} %iota_compare_fusion.1, bf16[16,128,512]{2,1,0:T(8,128)(2,1)} %param.18), kind=kOutput, calls=%fused_computation.24 | convolution fusion | flops 33946624 | bytes 2889728 | tf_op jit(solution)/shard_map/tgqd,tcgd->tgqc/dot_general | solution.py:26
  8.0 0.4 fusion.18
  8.5 0.0 copy-done.2
  8.5 0.0 copy-start.1
  8.5 0.8 fusion.15
  9.2 0.9 copy.48
  10.1 0.0 copy-done.1
  10.1 1.3 %copy.22.refs_4_ = bf16[4096,16]{1,0:T(8,128)(2,1)} copy(bf16[4096,16]{0,1:T(8,128)(2,1)S(1)} %copy-done.1) | data formatting | bytes 262144 | tf_op args[9]
  11.5 24.1 %shard_map.136 = (f32[16,4096]{1,0:T(8,128)}, bf16[16,4224]{1,0:T(8,128)(2,1)}) custom-call(bf16[16,8192]{1,0:T(8,128)(2,1)} %bitcast.40, bf16[1024,4096]{1,0:T(8,128)(2,1)} %refs_1_.2, bf16[16,4096]{1,0:T(8,128)(2,1)} %refs_2_.2, f32[1,4096]{1,0:T(1,128)} %bitcast.45, bf16[4096,16]{1,0:T(8,128)(2,1)} %copy.22.refs_4_, f32[16,16]{1,0:T(8,128)} %convert_element_type.35.refs_5_), custom_call_target="tpu_custom_call" | custom-call | tf_op jit(solution)/shard_map/pallas_call | solution.py:321
  35.6 0.0 copy-start
  35.6 63.8 %shard_map.137 = f32[16,4096]{1,0:T(8,128)} custom-call(bf16[16,4224]{1,0:T(8,128)(2,1)} %get-tuple-element.8.refs_0_, bf16[1,4096,384]{2,1,0:T(8,128)(2,1)} %refs_1_.3, bf16[1,4096,384]{2,1,0:T(8,128)(2,1)} %refs_2_.3, bf16[1,384,4096]{2,1,0:T(8,128)(2,1)} %refs_3_.1), custom_call_target="tpu_custom_call" | custom-call | tf_op jit(solution)/shard_map/pallas_call | solution.py:511
  99.4 0.0 copy-done
  99.4 1.7 %add.11 = f32[16,4096]{1,0:T(8,128)} add(f32[16,4096]{1,0:T(8,128)S(1)} %copy-done, f32[16,4096]{1,0:T(8,128)} %shard_map.137) | non-fusion elementwise | flops 65536 | bytes 786432 | tf_op jit(solution)/shard_map/add | solution.py:562
  (2 shorter events, 0.1 us)
Async XLA Ops:
  4.7 3.8 %copy-start.2 = (bf16[16,128,512]{2,1,0:T(8,128)(2,1)S(1)}, bf16[16,128,512]{2,1,0:T(8,128)(2,1)}, u32[]{:S(2)}) copy-start(bf16[16,128,512]{2,1,0:T(8,128)(2,1)} %param.19) | copy-start | bytes 6291460
  8.5 1.6 %copy-start.1 = (bf16[4096,16]{0,1:T(8,128)(2,1)S(1)}, bf16[4096,16]{0,1:T(8,128)(2,1)}, u32[]{:S(2)}) copy-start(bf16[4096,16]{0,1:T(8,128)(2,1)} %param.23) | copy-start | bytes 393220
  35.6 63.9 %copy-start = (f32[16,4096]{1,0:T(8,128)S(1)}, f32[16,4096]{1,0:T(8,128)}, u32[]{:S(2)}) copy-start(f32[16,4096]{1,0:T(8,128)} %get-tuple-element.7) | copy-start | bytes 786436
where the time goes:
time: 102 us; the launch traced here: 101 us
  Pallas kernels  88 us (86%)
  local copies, waits for them, and re-layouts  5.45 us (5%)
  matrix products  4.03 us (4%)
  other arithmetic  3.6 us (4%)
    pallas_call x1, Pallas kernels, run_experts(): pl.pallas_call(lambda *refs: expert_kernel(side, depth, *refs), out_shape...  63.8 us
    pallas_call x1, Pallas kernels, project(): pl.pallas_call(lambda *refs: projection_kernel(side, *refs), out_shape=(j...  24.1 us
    unnamed x10, local copies, waits for them, and re-layouts  3.99 us
    dot_general x1, matrix products, attend(): jnp.einsum('tgqd,tcgd->tgqc', query_heads, past_keys, preferred_element_t...  3.03 us

commit v1 on v0

v1 whole, which is shorter than its diff:
```python
import math

import jax
import jax.numpy as jnp
from jax import lax
from jax.experimental import pallas as pl
from jax.experimental.pallas import tpu as pltpu
from jax.sharding import PartitionSpec as P

D = 4096
H = 64
KVH = 4
HD = 128
TOP = 8


def attend(queries, new_keys, new_values, cache_keys, cache_values, cache_len):
    local_rows = queries.shape[0]
    cache_span = cache_keys.shape[1]
    group_size = H // KVH
    query_heads = queries.reshape(local_rows, KVH, group_size, HD)
    past_keys = cache_keys.reshape(local_rows, cache_span, KVH, HD)
    past_values = cache_values.reshape(local_rows, cache_span, KVH, HD)
    score_scale = 1.0 / math.sqrt(HD)
    past_scores = (
        jnp.einsum("tgqd,tcgd->tgqc", query_heads, past_keys, preferred_element_type=jnp.float32)
        * score_scale
    )
    own_scores = (
        jnp.einsum(
            "tgqd,tgd->tgq",
            query_heads,
            new_keys.reshape(local_rows, KVH, HD),
            preferred_element_type=jnp.float32,
        )
        * score_scale
    )
    is_valid = lax.broadcasted_iota(jnp.int32, (local_rows, cache_span), 1) < cache_len[:, None]
    past_scores = jnp.where(is_valid[:, None, None, :], past_scores, -1e30)
    peak_score = jnp.maximum(jnp.max(past_scores, axis=3), own_scores)
    past_exp = jnp.exp(past_scores - peak_score[..., None])
    own_exp = jnp.exp(own_scores - peak_score)
    denom_sum = jnp.sum(past_exp, axis=3) + own_exp
    past_weights = (past_exp / denom_sum[..., None]).astype(jnp.bfloat16)
    own_weights = (own_exp / denom_sum).astype(jnp.bfloat16)
    blended = jnp.einsum(
        "tgqc,tcgd->tgqd", past_weights, past_values, preferred_element_type=jnp.float32
    )
    blended = blended + own_weights.astype(jnp.float32)[..., None] * new_values.reshape(
        local_rows, KVH, 1, HD
    ).astype(jnp.float32)
    return blended.reshape(local_rows, H * HD).astype(jnp.bfloat16)


MESH = pl.DeviceIdType.MESH
VMEM_LIMIT = 66_000_000


class Place:
    def __init__(self, side, depth):
        self.side, self.depth = side, depth
        ep = lax.axis_index("ep")
        self.ep = ep
        self.core = lax.rem(ep, 2)
        self.x = lax.rem(ep // 2, side)
        self.y = ep // (2 * side)
        self.z = lax.axis_index("dp")

    def at(self, dy=0, dx=0, dz=0, flip=False):
        y, x = self.line(dy, dx)
        z = lax.rem(self.z + dz, self.depth) if dz else self.z
        core = 1 - self.core if flip else self.core
        return ((y * self.side + x) * 2 + core, z)

    def line(self, dy, dx):
        return lax.rem(self.y + dy, self.side), lax.rem(self.x + dx, self.side)


def greet(devices):
    barrier = pltpu.get_barrier_semaphore()
    for device in devices:
        pl.semaphore_signal(barrier, inc=1, device_id=device, device_id_type=MESH)
    pl.semaphore_wait(barrier, len(devices))


def remote(src, dst, send, recv, device):
    return pltpu.make_async_remote_copy(
        src_ref=src, dst_ref=dst, send_sem=send, recv_sem=recv, device_id=device, device_id_type=MESH
    )


def slices_of(width, extra=0):
    step = 512
    cuts = [[start, step] for start in range(0, width, step)]
    cuts[-1][1] += extra
    return cuts


def reduce_shapes(side, depth, rows, width):
    n = width // 512
    lines = side * side
    bf, dma = jnp.bfloat16, pltpu.SemaphoreType.DMA
    tall = depth * rows
    return [
        pltpu.VMEM((side, side, tall, width), bf),
        pltpu.VMEM((side - 1, side, tall, width), bf),
        pltpu.VMEM((side - 1, tall, width), bf),
        pltpu.VMEM((max(depth - 1, 1), rows, width), bf),
        dma((n, 2)),
        dma((n, side, side, 2)),
        dma((n, side, 2)),
        dma((n, depth, 2)),
    ]


def reduce_phases(here, rows, width, produce, finish, part, scratch, sends):
    in1, in2, in3, in4, sem1, sem2, sem3, sem4 = scratch
    side, depth = here.side, here.depth
    cuts = slices_of(width)

    def rows_of(z):
        return pl.ds(pl.multiple_of(z * rows, rows), rows)

    def core_copy(s):
        start, size = cuts[s]
        cols = pl.ds(start, size)
        return remote(
            part.at[:, :, 1 - here.core, :, cols],
            in1.at[:, :, :, cols],
            sem1.at[s, 0],
            sem1.at[s, 1],
            here.at(flip=True),
        )

    def offsets(s, a, b):
        return (a, b) if s % 2 == 0 else (b, a)

    def first_copy(s, ja, kb, sending):
        cols = pl.ds(*cuts[s])
        slot = side - ja - 1
        y, x = here.line(*offsets(s, ja, kb))
        return remote(
            in1.at[y, x, :, cols],
            in2.at[slot, kb, :, cols],
            sem2.at[s, ja, kb, 0],
            sem2.at[s, side - ja if sending else ja, kb, 1],
            here.at(*offsets(s, ja, 0)),
        )

    def second_copy(s, kb, sending):
        cols = pl.ds(*cuts[s])
        y, x = here.line(*offsets(s, 0, kb))
        return remote(
            in1.at[y, x, :, cols],
            in3.at[side - kb - 1, :, cols],
            sem3.at[s, kb, 0],
            sem3.at[s, side - kb if sending else kb, 1],
            here.at(*offsets(s, 0, kb)),
        )

    def depth_copy(s, jz, sending):
        cols = pl.ds(*cuts[s])
        return remote(
            in1.at[here.y, here.x, rows_of(lax.rem(here.z + jz, depth)), cols],
            in4.at[depth - jz - 1, :, cols],
            sem4.at[s, jz, 0],
            sem4.at[s, depth - jz if sending else jz, 1],
            here.at(0, 0, jz),
        )

    def go(copy):
        copy.start()
        sends.append(copy)

    def wide(value):
        return value.astype(jnp.float32)

    def phase0(s):
        cols = pl.ds(*cuts[s])
        value = produce(s, cols)
        part[:, :, :, :, cols] = value.astype(jnp.bfloat16).reshape(
            side, side, 2, depth * rows, cuts[s][1]
        )
        go(core_copy(s))

    def phase1(s):
        cols = pl.ds(*cuts[s])
        core_copy(s).wait_recv()
        for a in list(range(1, side)) + [0]:
            for b in list(range(1, side)) + [0]:
                y, x = here.line(*offsets(s, a, b))
                total = wide(part[y, x, here.core, :, cols]) + wide(in1[y, x, :, cols])
                in1[y, x, :, cols] = total.astype(jnp.bfloat16)
                if a:
                    go(first_copy(s, a, b, True))

    def phase2(s):
        cols = pl.ds(*cuts[s])
        for b in list(range(1, side)) + [0]:
            y, x = here.line(*offsets(s, 0, b))
            total = wide(in1[y, x, :, cols])
            for a in range(1, side):
                first_copy(s, a, b, False).wait_recv()
                total = total + wide(in2[a - 1, b, :, cols])
            in1[y, x, :, cols] = total.astype(jnp.bfloat16)
            if b:
                go(second_copy(s, b, True))

    def phase3(s):
        cols = pl.ds(*cuts[s])
        total = wide(in1[here.y, here.x, :, cols])
        for b in range(1, side):
            second_copy(s, b, False).wait_recv()
            total = total + wide(in3[b - 1, :, cols])
        if depth == 1:
            finish(s, cols, total)
            return
        in1[here.y, here.x, :, cols] = total.astype(jnp.bfloat16)
        for jz in range(1, depth):
            go(depth_copy(s, jz, True))

    def phase4(s):
        cols = pl.ds(*cuts[s])
        total = wide(in1[here.y, here.x, rows_of(here.z), cols])
        for jz in range(1, depth):
            depth_copy(s, jz, False).wait_recv()
            total = total + wide(in4[jz - 1, :, cols])
        finish(s, cols, total)

    if depth == 1:
        return phase0, phase1, phase2, phase3
    return phase0, phase1, phase2, phase3, phase4


def gather_phases(here, held, rows, width, extra, consume, zsem, lsem, csem, send_sem, sends):
    side, depth = here.side, here.depth
    cuts = slices_of(width, extra)

    def rows_of(z):
        return pl.ds(pl.multiple_of(z * rows, rows), rows)

    def go(copy):
        copy.start()
        sends.append(copy)

    def depth_copy(s, j, sending):
        z = here.z if sending else lax.rem(here.z + j, depth)
        ref = held.at[here.y, here.x, here.core, rows_of(z), pl.ds(*cuts[s])]
        return remote(
            ref, ref, zsem.at[s, j, 0], zsem.at[s, depth - j if sending else j, 1], here.at(0, 0, j)
        )

    def line_ref(s, ky, kx, core):
        y, x = here.line(ky, kx)
        return held.at[y, x, core, :, pl.ds(*cuts[s])]

    def plane_send(s, ky, kx, jy, jx):
        ref = line_ref(s, ky, kx, here.core)
        go(
            remote(
                ref,
                ref,
                send_sem.at[s, ky, kx, jy, jx],
                lsem.at[s, (ky - jy) % side, (kx - jx) % side],
                here.at(jy, jx),
            )
        )

    def core_send(s, ky, kx):
        ref = line_ref(s, ky, kx, here.core)
        go(remote(ref, ref, csem.at[s, ky, kx, 0], csem.at[s, ky, kx, 1], here.at(flip=True)))

    def plane_wait(s, ky, kx):
        ref = line_ref(s, ky, kx, here.core)
        remote(ref, ref, send_sem.at[s, 0, 0, 0, 0], lsem.at[s, ky, kx], here.at(flip=True)).wait_recv()

    def core_wait(s, ky, kx):
        ref = line_ref(s, ky, kx, 1 - here.core)
        remote(ref, ref, csem.at[s, ky, kx, 0], csem.at[s, ky, kx, 1], here.at(flip=True)).wait_recv()

    def turn(s, a, b):
        return (a, b) if s % 2 == 0 else (b, a)

    def phase1(s):
        for j in range(1, depth):
            depth_copy(s, j, False).wait_recv()
        for j in range(1, side):
            plane_send(s, 0, 0, *turn(s, j, 0))
            plane_send(s, 0, 0, *turn(s, 0, j))
        core_send(s, 0, 0)

    def phase2(s):
        for k in range(1, side):
            plane_wait(s, *turn(s, k, 0))
            for j in range(1, side):
                plane_send(s, *turn(s, k, 0), *turn(s, 0, j))
            core_send(s, *turn(s, k, 0))

    def phase3(s):
        for b in range(1, side):
            for a in range(side):
                plane_wait(s, *turn(s, a, b))
                core_send(s, *turn(s, a, b))

    def phase0(s):
        for j in range(1, depth):
            go(depth_copy(s, j, True))

    def phase4(s):
        for a in range(side):
            for b in range(side):
                core_wait(s, a, b)
        consume(s)

    return phase0, phase1, phase2, phase3, phase4


def run_in_order(groups):
    tasks = []
    for phases, count, starts, paces in groups:
        last = [-1.0] * count
        for phase, start, pace in zip(phases, starts, paces):
            for s in range(count):
                last[s] = max(last[s] + 1e-6, start + pace * s)
                tasks.append((last[s], len(tasks), phase, s))
    for _, _, phase, s in sorted(tasks, key=lambda task: task[:2]):
        phase(s)


def layer_kernel(
    side, depth, attended, resid, gain, router, named_ids, proj_hbm, gate_hbm, up_hbm, down_hbm, mixed,
    proj, gate, up, down, regrouped, part, hidden, held, act, gate_sum, up_sum,
    wsem, ssem, rsem, zsem, lsem, csem, send_sem, *scratch
):
    here, flat = Place(side, depth), Place(side, 1)
    rows, features = resid.shape
    experts = router.shape[0]
    count = 2 * side * side
    width = attended.shape[1] // count
    loads = [
        pltpu.make_async_copy(src, dst, wsem.at[i])
        for i, (src, dst) in enumerate(
            ((proj_hbm, proj), (gate_hbm.at[0], gate), (up_hbm.at[0], up), (down_hbm.at[0], down))
        )
    ]
    for load in loads:
        load.start()

    def peer(j):
        return lax.rem(here.ep + j, count)

    greet([(peer(j), here.z) for j in range(1, count)] + [here.at(0, 0, j) for j in range(1, depth)])

    def piece(index):
        return attended.at[:, pl.ds(pl.multiple_of(index * width, 128), width)]

    def exchange(j, sending):
        return remote(
            piece(peer(j)),
            regrouped.at[here.ep] if sending else regrouped.at[peer(j)],
            ssem.at[j],
            rsem.at[count - j if sending else j],
            (peer(j), here.z),
        )

    sends = [exchange(j, True) for j in range(1, count)]
    for copy in sends:
        copy.start()
    regrouped[here.ep] = attended[:, pl.ds(pl.multiple_of(here.ep * width, 128), width)]

    eye = jnp.where(
        lax.broadcasted_iota(jnp.int32, (rows, rows), 0) == lax.broadcasted_iota(jnp.int32, (rows, rows), 1), 1.0, 0.0
    ).astype(jnp.bfloat16)
    label = lax.broadcasted_iota(jnp.int32, (experts, rows), 0)
    hits = jnp.zeros((experts, rows), jnp.float32)
    for k in range(TOP):
        hits = hits + jnp.where(label == named_ids[k : k + 1, :], 1.0, 0.0)
    named = nt_dot(eye, hits.astype(jnp.bfloat16)) > 0.5

    loads[0].wait()
    for j in range(1, count):
        exchange(j, False).wait_recv()

    def produce_proj(s, cols):
        left = regrouped[...].reshape(count * rows, width)
        return jnp.dot(left, proj[:, cols], preferred_element_type=jnp.float32)

    squares, logits = [], []
    slices = len(slices_of(features))
    tail_width = held.shape[-1] - features
    mine = pl.ds(pl.multiple_of(here.z * rows, rows), rows)

    def finish_proj(s, cols, total):
        value = resid[:, cols].astype(jnp.float32) + total
        hidden[:, cols] = value
        scaled = (value * gain[:, cols]).astype(jnp.bfloat16)
        held[here.y, here.x, here.core, mine, cols] = scaled
        if s < slices - 1:
            gather[0](s)
        squares.append(jnp.sum(value * value, axis=1, keepdims=True))
        logits.append(nt_dot(scaled, router[:, cols]))
        if s == slices - 1:
            scale = lax.rsqrt(jnp.maximum(sum(squares) / features, 0.25))
            scores = sum(logits) * scale
            peak = jnp.max(jnp.where(named, scores, -jnp.inf), axis=1, keepdims=True)
            grown = jnp.where(named, jnp.exp(jnp.where(named, scores - peak, 0.0)), 0.0)
            probs = grown / jnp.sum(grown, axis=1, keepdims=True)
            high = scale.astype(jnp.bfloat16).astype(jnp.float32)
            lane = lax.broadcasted_iota(jnp.int32, (rows, tail_width), 1)
            tail = jnp.where(lane == experts, high, jnp.where(lane == experts + 1, scale - high, 0.0))
            held[here.y, here.x, here.core, mine, features:] = tail.astype(jnp.bfloat16)
            held[here.y, here.x, here.core, mine, features : features + experts] = probs.astype(jnp.bfloat16)
            gather[0](s)

    group = side * 2 * depth * rows

    def rows_at(y):
        return pl.ds(pl.multiple_of(y * group, group), group)

    def consume(s):
        if s == 0:
            loads[1].wait()
            loads[2].wait()
        start = 512 * s

        def step(y, carry):
            block = held[y, :, :, :, start : start + 512].reshape(group, 512)
            for weight, total in ((gate, gate_sum), (up, up_sum)):
                value = jnp.dot(
                    block, weight[start : start + 512, :], preferred_element_type=jnp.float32
                )
                total[rows_at(y), :] = value if s == 0 else total[rows_at(y), :] + value
            return carry

        lax.fori_loop(0, side, step, 0)

    proj_scratch, expert_scratch = scratch[: len(scratch) // 2], scratch[len(scratch) // 2 :]
    reduce = reduce_phases(flat, rows, features, produce_proj, finish_proj, part, proj_scratch, sends)
    gather = gather_phases(
        here, held, rows, features, tail_width, consume, zsem, lsem, csem, send_sem, sends
    )
    run_in_order(
        (
            (reduce, slices, PROJ_START, PROJ_PACE),
            (gather[1:], slices, GATHER_START, GATHER_PACE),
        )
    )
    loads[3].wait()
    for copy in sends:
        copy.wait_send()
    sends.clear()
    expert = (here.ep * depth + here.z) // 2

    def activate(y, carry):
        tail = held[y, :, :, :, features:].reshape(group, tail_width).astype(jnp.float32)
        lane = lax.broadcasted_iota(jnp.int32, tail.shape, 1)
        weight = jnp.sum(jnp.where(lane == expert, tail, 0.0), axis=1, keepdims=True)
        scale = jnp.sum(
            jnp.where((lane == experts) | (lane == experts + 1), tail, 0.0), axis=1, keepdims=True
        )
        gate_val = gate_sum[rows_at(y), :] * scale
        value = gate_val / (1.0 + jnp.exp(-gate_val)) * (up_sum[rows_at(y), :] * (scale * weight))
        act[rows_at(y), :] = value.astype(jnp.bfloat16)
        return carry

    lax.fori_loop(0, side, activate, 0)

    def produce(s, cols):
        return jnp.dot(act[...], down[:, cols], preferred_element_type=jnp.float32)

    def finish(s, cols, total):
        mixed[:, cols] = hidden[:, cols] + total

    spread = reduce_phases(here, rows, features, produce, finish, held, expert_scratch, sends)
    run_in_order(((spread, slices, SPREAD_START, SPREAD_PACE),))
    for copy in sends:
        copy.wait_send()


PROJ_START, PROJ_PACE = (0.0, 1.5, 4.5, 7.5), (0.3, 0.5, 0.5, 0.5)
GATHER_START, GATHER_PACE = (11.5, 14.5, 16.5, 18.0), (1.2, 1.75, 1.75, 1.75)
SPREAD_START, SPREAD_PACE = (0.0, 1.5, 5.0, 8.0, 12.0), (0.5, 1.75, 1.75, 1.75, 1.75)


def nt_dot(left, right):
    return lax.dot_general(left, right, (((1,), (1,)), ((), ())), preferred_element_type=jnp.float32)


def run_layer(side, depth, attended, resid, gain, router, named_ids, out_proj, gate_slab, up_slab, down_slab):
    rows, width = resid.shape
    n = width // 512
    experts = router.shape[0]
    bf, dma = jnp.bfloat16, pltpu.SemaphoreType.DMA
    plane = 2 * side * side
    count = plane * depth
    tail = pl.cdiv(experts + 2, 128) * 128
    vmem, anywhere = pl.BlockSpec(memory_space=pltpu.VMEM), pl.BlockSpec(memory_space=pl.ANY)
    return pl.pallas_call(
        lambda *refs: layer_kernel(side, depth, *refs),
        out_shape=jax.ShapeDtypeStruct((rows, width), jnp.float32),
        in_specs=[vmem] * 5 + [anywhere] * 4,
        out_specs=vmem,
        scratch_shapes=[
            pltpu.VMEM(out_proj.shape, bf),
            pltpu.VMEM(gate_slab.shape[1:], bf),
            pltpu.VMEM(up_slab.shape[1:], bf),
            pltpu.VMEM(down_slab.shape[1:], bf),
            pltpu.VMEM((plane, rows, attended.shape[1] // plane), bf),
            pltpu.VMEM((side, side, 2, rows, width), bf),
            pltpu.VMEM((rows, width), jnp.float32),
            pltpu.VMEM((side, side, 2, depth * rows, width + tail), bf),
            pltpu.VMEM((count * rows, gate_slab.shape[2]), bf),
            pltpu.VMEM((count * rows, gate_slab.shape[2]), jnp.float32),
            pltpu.VMEM((count * rows, gate_slab.shape[2]), jnp.float32),
            dma((4,)),
            dma((plane,)),
            dma((plane,)),
            dma((n, depth, 2)),
            dma((n, side, side)),
            dma((n, side, side, 2)),
            dma((n, side, side, side, side)),
        ]
        + reduce_shapes(side, 1, rows, width)
        + reduce_shapes(side, depth, rows, width),
        compiler_params=pltpu.CompilerParams(
            collective_id=0, has_side_effects=True, vmem_limit_bytes=VMEM_LIMIT
        ),
    )(attended, resid, gain, router, named_ids, out_proj, gate_slab, up_slab, down_slab)


def local(
    resid,
    queries,
    new_keys,
    new_values,
    cache_keys,
    cache_values,
    cache_len,
    out_proj,
    norm_gain,
    router,
    expert_ids,
    gate_slab,
    up_slab,
    down_slab,
):
    attended = attend(queries, new_keys, new_values, cache_keys, cache_values, cache_len)
    side = math.isqrt(lax.axis_size("ep") // 2)
    depth = lax.axis_size("dp")
    return run_layer(
        side, depth, attended, resid, norm_gain.reshape(1, -1), router.T, expert_ids.T,
        out_proj, gate_slab, up_slab, down_slab,
    )


def solution(mesh):
    in_specs = (
        P(("ep", "dp"), None),
        P(("ep", "dp"), None),
        P(("ep", "dp"), None),
        P(("ep", "dp"), None),
        P(("ep", "dp"), None, None),
        P(("ep", "dp"), None, None),
        P(("ep", "dp")),
        P("ep", None),
        P(),
        P(),
        P(("ep", "dp"), None),
        P(("ep", "dp"), None, None),
        P(("ep", "dp"), None, None),
        P(("ep", "dp"), None, None),
    )
    out_specs = P(("ep", "dp"), None)
    return jax.shard_map(local, mesh=mesh, in_specs=in_specs, out_specs=out_specs, check_vma=False)
```

time: 102 us -> 92.6 us (0.908)
  Pallas kernels: 88 us -> 81.9 us
  other arithmetic: 3.6 us -> 1.21 us
    pallas_call x2 -> x1, Pallas kernels: 88 us -> 81.9 us  [run_layer(): pl.pallas_call(lambda *refs: layer_kernel(side, depth, *refs), out_shape=...]
    add x1 -> x0, other arithmetic: 1.69 us -> none  [local(): hidden + run_experts(side, depth, packed, gate_slab, up_slab, down_slab)]
    unnamed x10 -> x5, local copies, waits for them, and re-layouts: 3.99 us -> 3.55 us
where the time goes in v1:
time: 92.6 us; the launch traced here: 92.2 us
  Pallas kernels  81.9 us (88%)
  local copies, waits for them, and re-layouts  5.02 us (5%)
  matrix products  4.03 us (4%)
  other arithmetic  1.21 us (1%)
    pallas_call x1, Pallas kernels, run_layer(): pl.pallas_call(lambda *refs: layer_kernel(side, depth, *refs), out_shape=...  81.9 us
    unnamed x5, local copies, waits for them, and re-layouts  3.55 us
    dot_general x1, matrix products, attend(): jnp.einsum('tgqd,tcgd->tgqc', query_heads, past_keys, preferred_element_t...  3.03 us

profile of v1, /device:TPU:0, one launch (start us, length us, event | category | flops | bytes accessed | tf_op | source)
XLA Modules:
  0.0 92.2 jit_solution(8401629774167183050)
XLA Ops:
  0.0 0.7 iota_compare_fusion
  0.7 0.7 reshape.54
  1.5 0.7 reshape.50
  2.2 1.0 %copy.21 = bf16[2,8,64,128]{3,2,1,0:T(8,128)(2,1)S(1)} copy(bf16[2,8,64,128]{3,1,2,0:T(8,128)(2,1)} %bitcast.43) | data formatting | bytes 524288
  3.2 0.0 copy-start
  3.2 0.2 fusion.24
  3.5 3.0 %fusion.23 = (f32[16,4,16]{2,1,0:T(4,128)S(1)}, f32[16,4,16,128]{3,2,1,0:T(8,128)S(1)}) fusion(bf16[16,4,16,128]{3,2,1,0:T(8,128)(2,1)S(1)} %bitcast.42, pred[16,128]{1,0:T(8,128)(4,1)S(1)} %iota_compare_fusion, bf16[16,128,512]{2,1,0:T(8,128)(2,1)} %param.18), kind=kOutput, calls=%fused_computation.22 | convolution fusion | flops 33946624 | bytes 2889728 | tf_op jit(solution)/shard_map/tgqd,tcgd->tgqc/dot_general | solution.py:26
  6.5 0.4 fusion.18
  7.0 0.0 copy-done
  7.0 0.8 fusion.15
  7.8 0.9 copy.42
  8.6 81.9 %shard_map.136 = f32[16,4096]{1,0:T(8,128)} custom-call(bf16[16,8192]{1,0:T(8,128)(2,1)} %bitcast.40, bf16[16,4096]{1,0:T(8,128)(2,1)} %refs_1_.1, f32[1,4096]{1,0:T(1,128)} %bitcast.48, bf16[16,4096]{1,0:T(8,128)(2,1)} %bitcast.45, s32[8,16]{1,0:T(8,128)} %bitcast.49, bf16[1024,4096]{1,0:T(8,128)(2,1)} %refs_5_.1, bf16[1,4096,384]{2,1,0:T(8,128)(2,1)} %refs_6_.1, ...), custom_call_target="tpu_custom_call" | custom-call | tf_op jit(solution)/shard_map/pallas_call | solution.py:498
  90.5 1.7 %copy.44 = f32[16,4096]{1,0:T(8,128)} copy(f32[16,4096]{1,0:T(8,128)} %shard_map.136) | data formatting | bytes 524288
  (2 shorter events, 0.1 us)
Async XLA Ops:
  3.2 3.8 %copy-start = (bf16[16,128,512]{2,1,0:T(8,128)(2,1)S(1)}, bf16[16,128,512]{2,1,0:T(8,128)(2,1)}, u32[]{:S(2)}) copy-start(bf16[16,128,512]{2,1,0:T(8,128)(2,1)} %param.19) | copy-start | bytes 6291460

commit v2 on v1

v2 whole, which is shorter than its diff:
```python
import math

import jax
import jax.numpy as jnp
from jax import lax
from jax.experimental import pallas as pl
from jax.experimental.pallas import tpu as pltpu
from jax.sharding import PartitionSpec as P

D = 4096
H = 64
KVH = 4
HD = 128
TOP = 8


MESH = pl.DeviceIdType.MESH
VMEM_LIMIT = 67_000_000


class Place:
    def __init__(self, side, depth):
        self.side, self.depth = side, depth
        ep = lax.axis_index("ep")
        self.ep = ep
        self.core = lax.rem(ep, 2)
        self.x = lax.rem(ep // 2, side)
        self.y = ep // (2 * side)
        self.z = lax.axis_index("dp")

    def at(self, dy=0, dx=0, dz=0, flip=False):
        y, x = self.line(dy, dx)
        z = lax.rem(self.z + dz, self.depth) if dz else self.z
        core = 1 - self.core if flip else self.core
        return ((y * self.side + x) * 2 + core, z)

    def line(self, dy, dx):
        return lax.rem(self.y + dy, self.side), lax.rem(self.x + dx, self.side)


def announce(devices):
    barrier = pltpu.get_barrier_semaphore()
    for device in devices:
        pl.semaphore_signal(barrier, inc=1, device_id=device, device_id_type=MESH)


def gathered(devices):
    pl.semaphore_wait(pltpu.get_barrier_semaphore(), len(devices))


def remote(src, dst, send, recv, device):
    return pltpu.make_async_remote_copy(
        src_ref=src, dst_ref=dst, send_sem=send, recv_sem=recv, device_id=device, device_id_type=MESH
    )


def slices_of(width):
    sizes = [512] * (width // 512)
    sizes = [256, 256] + sizes[2:] + [256, 256]
    cuts, start = [], 0
    for size in sizes:
        cuts.append((start, size))
        start += size
    return cuts


def reduce_shapes(side, depth, rows, width):
    bf, tall = jnp.bfloat16, depth * rows
    return [
        pltpu.VMEM((side, side, tall, width), bf),
        pltpu.VMEM((side - 1, side, tall, width), bf),
        pltpu.VMEM((side - 1, tall, width), bf),
        pltpu.VMEM((max(depth - 1, 1), rows, width), bf),
    ]


def reduce_sems(side, n):
    dma = pltpu.SemaphoreType.DMA
    return [dma((4,)), dma((n,)), dma((n, side - 1, side)), dma((n, side - 1)), dma((n,))]


def wide(value):
    return value.astype(jnp.float32)


def wait_bytes(ref, sem):
    pltpu.make_async_copy(ref, ref, sem).wait()


def reduce_phases(here, rows, width, produce, finish, part, buffers, sems):
    in1, in2, in3, in4 = buffers
    sent, sem1, sem2, sem3, sem4 = sems
    side, depth = here.side, here.depth
    tall = depth * rows
    cuts = slices_of(width)

    def rows_of(z):
        return pl.ds(pl.multiple_of(z * rows, rows), rows)

    every = slice(None)

    def core_copy(s):
        cols = pl.ds(*cuts[s])
        return remote(
            part(every, every, 1 - here.core, cols),
            in1.at[:, :, :, cols],
            sent.at[0],
            sem1.at[s],
            here.at(flip=True),
        )

    def offsets(s, a, b):
        return (a, b) if s % 2 == 0 else (b, a)

    def first_copy(s, ja, kb, sending):
        cols = pl.ds(*cuts[s])
        slot = side - ja - 1
        y, x = here.line(*offsets(s, ja, kb))
        return remote(
            in1.at[y, x, :, cols],
            in2.at[slot, kb, :, cols],
            sent.at[1],
            sem2.at[s, (side - ja if sending else ja) - 1, kb],
            here.at(*offsets(s, ja, 0)),
        )

    def second_copy(s, kb, sending):
        cols = pl.ds(*cuts[s])
        y, x = here.line(*offsets(s, 0, kb))
        return remote(
            in1.at[y, x, :, cols],
            in3.at[side - kb - 1, :, cols],
            sent.at[2],
            sem3.at[s, (side - kb if sending else kb) - 1],
            here.at(*offsets(s, 0, kb)),
        )

    def depth_copy(s, jz):
        cols = pl.ds(*cuts[s])
        return remote(
            in1.at[here.y, here.x, rows_of(lax.rem(here.z + jz, depth)), cols],
            in4.at[depth - jz - 1, :, cols],
            sent.at[3],
            sem4.at[s],
            here.at(0, 0, jz),
        )

    def phase0(s):
        cols = pl.ds(*cuts[s])
        value = produce(s, cols).astype(jnp.bfloat16).reshape(side, side, 2, tall, cuts[s][1])
        for core in range(2):
            part(every, every, core, cols)[...] = value[:, :, core]
        core_copy(s).start()

    def phase1(s):
        cols = pl.ds(*cuts[s])
        core_copy(s).wait_recv()
        for a in list(range(1, side)) + [0]:
            for b in list(range(1, side)) + [0]:
                y, x = here.line(*offsets(s, a, b))
                total = wide(part(y, x, here.core, cols)[...]) + wide(in1[y, x, :, cols])
                in1[y, x, :, cols] = total.astype(jnp.bfloat16)
                if a:
                    first_copy(s, a, b, True).start()

    def phase2(s):
        cols = pl.ds(*cuts[s])
        for b in list(range(1, side)) + [0]:
            y, x = here.line(*offsets(s, 0, b))
            total = wide(in1[y, x, :, cols])
            for a in range(1, side):
                first_copy(s, a, b, False).wait_recv()
                total = total + wide(in2[a - 1, b, :, cols])
            in1[y, x, :, cols] = total.astype(jnp.bfloat16)
            if b:
                second_copy(s, b, True).start()

    def phase3(s):
        cols = pl.ds(*cuts[s])
        total = wide(in1[here.y, here.x, :, cols])
        for b in range(1, side):
            second_copy(s, b, False).wait_recv()
            total = total + wide(in3[b - 1, :, cols])
        if depth == 1:
            finish(s, cols, total)
            return
        in1[here.y, here.x, :, cols] = total.astype(jnp.bfloat16)
        for jz in range(1, depth):
            depth_copy(s, jz).start()

    def phase4(s):
        cols = pl.ds(*cuts[s])
        total = wide(in1[here.y, here.x, rows_of(here.z), cols])
        wait_bytes(in4.at[:, :, cols], sem4.at[s])
        for jz in range(1, depth):
            total = total + wide(in4[jz - 1, :, cols])
        finish(s, cols, total)

    def wait_core():
        wait_bytes(in1, sent.at[0])

    def wait_sent():
        wait_bytes(in1.at[0 : side - 1], sent.at[1])
        wait_bytes(in1.at[0, 0 : side - 1], sent.at[2])
        if depth > 1:
            wait_bytes(in1.at[0, 0, 0 : (depth - 1) * rows, :], sent.at[3])

    phases = phase0, phase1, phase2, phase3, phase4
    return phases[: 4 if depth == 1 else 5], wait_core, wait_sent


def gather_phases(here, held, rows, features, consume, sems):
    side, depth = here.side, here.depth
    sent, zsem, lsem, csem = sems
    cuts = slices_of(features)
    cuts[-1] = (cuts[-1][0], held.shape[-1] - cuts[-1][0])

    def rows_of(z):
        return pl.ds(pl.multiple_of(z * rows, rows), rows)

    def line_ref(s, ky, kx, core):
        y, x = here.line(ky, kx)
        return held.at[y, x, core, :, pl.ds(*cuts[s])]

    def arrival(s, ky, kx):
        return lsem.at[s, (ky % side) * side + kx % side - 1]

    def own_send(s, jz):
        ref = held.at[here.y, here.x, here.core, rows_of(lax.rem(here.z + jz, depth)), pl.ds(*cuts[s])]
        for j in range(1, side):
            for jy, jx in ((j, 0), (0, j)) if s % 2 == 0 else ((0, j), (j, 0)):
                remote(ref, ref, sent.at[1], arrival(s, -jy, -jx), here.at(jy, jx)).start()

    def core_send(s, ky, kx):
        ref = line_ref(s, ky, kx, here.core)
        remote(ref, ref, sent.at[3], csem.at[s], here.at(flip=True)).start()

    def plane_wait(s, ky, kx):
        wait_bytes(line_ref(s, ky, kx, here.core), arrival(s, ky, kx))

    def turn(s, a, b):
        return (a, b) if s % 2 == 0 else (b, a)

    def phase0(s):
        ref = held.at[here.y, here.x, here.core, rows_of(here.z), pl.ds(*cuts[s])]
        for j in range(1, depth):
            remote(ref, ref, sent.at[0], zsem.at[s], here.at(0, 0, j)).start()
        own_send(s, 0)

    def phase1(s):
        others = held.at[here.y, here.x, here.core, 0 : (depth - 1) * rows, pl.ds(*cuts[s])]
        wait_bytes(others, zsem.at[s])
        for j in range(1, depth):
            own_send(s, j)
        core_send(s, 0, 0)

    def phase2(s):
        for k in range(1, side):
            plane_wait(s, *turn(s, k, 0))
            ref = line_ref(s, *turn(s, k, 0), here.core)
            for j in range(1, side):
                jy, jx = turn(s, 0, j)
                ky, kx = turn(s, k, 0)
                remote(ref, ref, sent.at[2], arrival(s, ky - jy, kx - jx), here.at(jy, jx)).start()
            core_send(s, *turn(s, k, 0))

    def phase3(s):
        for b in range(1, side):
            for a in range(side):
                plane_wait(s, *turn(s, a, b))
                core_send(s, *turn(s, a, b))

    def phase4(s):
        wait_bytes(held.at[:, :, 1 - here.core, :, pl.ds(*cuts[s])], csem.at[s])
        consume(s)

    def wait_sent():
        if depth > 1:
            wait_bytes(held.at[0, 0, 0, 0 : (depth - 1) * rows, :], sent.at[0])
        wait_bytes(held.at[0 : side - 1, 0:2, 0], sent.at[1])
        wait_bytes(held.at[0 : side - 1, 0 : side - 1, 0], sent.at[2])
        wait_bytes(held.at[:, :, 0], sent.at[3])

    return (phase0, phase1, phase2, phase3, phase4), wait_sent


def run_in_order(groups):
    tasks = []
    for phases, count, keys in groups:
        last = [-1.0] * count
        for phase, (start, burst, quick, pace) in zip(phases, keys):
            for s in range(count):
                last[s] = max(last[s] + 1e-6, start + quick * min(s, burst) + pace * max(0, s - burst))
                tasks.append((last[s], len(tasks), phase, s))
    for _, _, phase, s in sorted(tasks, key=lambda task: task[:2]):
        phase(s)


def layer_kernel(
    side, depth, lengths, queries, new_keys, new_values, resid, gain, router, named_ids,
    keys_hbm, values_hbm, proj_hbm, gate_hbm, up_hbm, down_hbm, mixed,
    keys, values, query_rows, blend_rows, attended,
    proj, gate, up, down, regrouped, hidden, held, act, gate_sum, up_sum,
    ksem, wsem, xsem, *scratch
):
    here, flat = Place(side, depth), Place(side, 1)
    rows, features = resid.shape
    experts = router.shape[0]
    count = 2 * side * side
    width = attended.shape[1] // count
    span = keys_hbm.shape[1]
    group_size = H // KVH
    pieces = count // KVH
    own_group = here.ep // pieces

    def peer(j):
        return lax.rem(here.ep + j, count)

    peers = [(peer(j), here.z) for j in range(1, count)] + [here.at(0, 0, j) for j in range(1, depth)]
    announce(peers)

    def turn_group(i):
        return lax.rem(own_group + 1 + i, KVH)

    def lanes(g):
        return pl.ds(pl.multiple_of(g * HD, HD), HD)

    def cache_copies(i):
        return [
            pltpu.make_async_copy(
                src.at[:, :, lanes(turn_group(i))], dst.at[:, 0:span, lanes(turn_group(i))], ksem.at[n, i]
            )
            for n, (src, dst) in enumerate(((keys_hbm, keys), (values_hbm, values)))
        ]

    for i in range(KVH):
        for copy in cache_copies(i):
            copy.start()
    loads = [
        pltpu.make_async_copy(src, dst, wsem.at[i])
        for i, (src, dst) in enumerate(
            ((proj_hbm, proj), (gate_hbm.at[0], gate), (up_hbm.at[0], up), (down_hbm.at[0], down))
        )
    ]
    loads[0].start()

    first = lax.broadcasted_iota(jnp.int32, (PAD, KVH * HD), 0) == 0
    for new, cache in ((new_keys, keys), (new_values, values)):
        wide_new = new[...].astype(jnp.float32)
        for token in range(rows):
            own = jnp.where(first, wide_new[token : token + 1, :], 0.0)
            cache[token, span:, :] = own.astype(jnp.bfloat16)

    def piece(index):
        return attended.at[:, pl.ds(pl.multiple_of(index * width, 128), width)]

    def exchange(to, source):
        return remote(piece(to), regrouped.at[source], xsem.at[0], xsem.at[1], (to, here.z))

    def attend(i):
        g = turn_group(i)
        for copy in cache_copies(i):
            copy.wait()
        for h in range(group_size):
            query_rows[h * rows : (h + 1) * rows, :] = wide(queries[:, lanes(g * group_size + h)])
        scores = []
        place = lax.broadcasted_iota(jnp.int32, (group_size, span + PAD), 1)
        for token in range(rows):
            query = query_rows[pl.ds(token, group_size, stride=rows), :]
            score = nt_dot(query.astype(jnp.bfloat16), keys[token, :, lanes(g)])
            kept = (place < lengths[token]) | (place == span)
            scores.append(jnp.where(kept, score * (1.0 / math.sqrt(HD)), -1e30))
        score = jnp.concatenate(scores, axis=0)
        grown = jnp.exp(score - jnp.max(score, axis=1, keepdims=True))
        weights = (grown / jnp.sum(grown, axis=1, keepdims=True)).astype(jnp.bfloat16)
        for token in range(rows):
            blend_rows[pl.ds(token, group_size, stride=rows), :] = jnp.dot(
                weights[token * group_size : (token + 1) * group_size, :],
                values[token, :, lanes(g)],
                preferred_element_type=jnp.float32,
            )
        for h in range(group_size):
            attended[:, lanes(g * group_size + h)] = blend_rows[h * rows : (h + 1) * rows, :].astype(
                jnp.bfloat16
            )

    for i in range(KVH):
        if i == KVH - 1:
            gathered(peers)
            for load in loads[1:]:
                load.start()
            for sent in range(i):
                for k in range(pieces):
                    exchange(turn_group(sent) * pieces + k, here.ep).start()
        attend(i)
    for k in range(1, pieces):
        exchange(own_group * pieces + lax.rem(here.ep + k, pieces), here.ep).start()
    regrouped[here.ep] = attended[:, pl.ds(pl.multiple_of(here.ep * width, 128), width)]

    eye = jnp.where(
        lax.broadcasted_iota(jnp.int32, (rows, rows), 0) == lax.broadcasted_iota(jnp.int32, (rows, rows), 1), 1.0, 0.0
    ).astype(jnp.bfloat16)
    label = lax.broadcasted_iota(jnp.int32, (experts, rows), 0)
    hits = jnp.zeros((experts, rows), jnp.float32)
    for k in range(TOP):
        hits = hits + jnp.where(label == named_ids[k : k + 1, :], 1.0, 0.0)
    named = nt_dot(eye, hits.astype(jnp.bfloat16)) > 0.5

    loads[0].wait()
    with jax.named_scope("exchange_wait"):
        wait_bytes(regrouped.at[0 : count - 1], xsem.at[1])

    def produce_proj(s, cols):
        left = regrouped[...].reshape(count * rows, width)
        return jnp.dot(left, proj[:, cols], preferred_element_type=jnp.float32)

    squares, logits = [], []
    slices = len(slices_of(features))
    tail_width = held.shape[-1] - features
    mine = pl.ds(pl.multiple_of(here.z * rows, rows), rows)

    def finish_proj(s, cols, total):
        value = resid[:, cols].astype(jnp.float32) + total
        hidden[:, cols] = value
        scaled = (value * gain[:, cols]).astype(jnp.bfloat16)
        held[here.y, here.x, here.core, mine, cols] = scaled
        if s < slices - 1:
            gather[0](s)
        squares.append(jnp.sum(value * value, axis=1, keepdims=True))
        logits.append(nt_dot(scaled, router[:, cols]))
        if s == slices - 1:
            scale = lax.rsqrt(jnp.maximum(sum(squares) / features, 0.25))
            scores = sum(logits) * scale
            peak = jnp.max(jnp.where(named, scores, -jnp.inf), axis=1, keepdims=True)
            grown = jnp.where(named, jnp.exp(jnp.where(named, scores - peak, 0.0)), 0.0)
            probs = grown / jnp.sum(grown, axis=1, keepdims=True)
            high = scale.astype(jnp.bfloat16).astype(jnp.float32)
            lane = lax.broadcasted_iota(jnp.int32, (rows, tail_width), 1)
            tail = jnp.where(lane == experts, high, jnp.where(lane == experts + 1, scale - high, 0.0))
            held[here.y, here.x, here.core, mine, features:] = tail.astype(jnp.bfloat16)
            held[here.y, here.x, here.core, mine, features : features + experts] = probs.astype(jnp.bfloat16)
            gather[0](s)

    group = side * 2 * depth * rows

    def rows_at(y):
        return pl.ds(pl.multiple_of(y * group, group), group)

    def consume(s):
        if s == 0:
            loads[1].wait()
            loads[2].wait()
        start, size = slices_of(features)[s]

        def step(y, carry):
            block = held[y, :, :, :, start : start + size].reshape(group, size)
            for weight, total in ((gate, gate_sum), (up, up_sum)):
                value = jnp.dot(
                    block, weight[start : start + size, :], preferred_element_type=jnp.float32
                )
                total[rows_at(y), :] = value if s == 0 else total[rows_at(y), :] + value
            return carry

        lax.fori_loop(0, side, step, 0)

    proj_buffers, expert_buffers, rest = scratch[:4], scratch[4:8], scratch[8:]
    proj_sems, expert_sems, gather_sems = rest[:5], rest[5:10], rest[10:]
    def rows_of(block):
        return pl.ds(block * rows if isinstance(block, int) else pl.multiple_of(block * rows, rows), rows)

    def proj_parts(y, x, core, cols):
        return expert_buffers[0].at[y, x, rows_of(core), cols]

    reduce, wait_core, wait_reduce = reduce_phases(
        flat, rows, features, produce_proj, finish_proj, proj_parts, proj_buffers, proj_sems
    )
    gather, wait_gather = gather_phases(here, held, rows, features, consume, gather_sems)

    def finish_core(s):
        wait_core()

    run_in_order(
        (
            (reduce, slices, PROJ_KEYS),
            ((finish_core,), 1, (PROJ_KEYS[3],)),
            (gather[1:], slices, GATHER_KEYS),
        )
    )
    loads[3].wait()
    with jax.named_scope("drain_gather"):
        wait_reduce()
        wait_gather()
        wait_bytes(regrouped.at[0 : count - 1], xsem.at[0])
    expert = (here.ep * depth + here.z) // 2

    def activate(y, carry):
        tail = held[y, :, :, :, features:].reshape(group, tail_width).astype(jnp.float32)
        lane = lax.broadcasted_iota(jnp.int32, tail.shape, 1)
        weight = jnp.sum(jnp.where(lane == expert, tail, 0.0), axis=1, keepdims=True)
        scale = jnp.sum(
            jnp.where((lane == experts) | (lane == experts + 1), tail, 0.0), axis=1, keepdims=True
        )
        gate_val = gate_sum[rows_at(y), :] * scale
        value = gate_val / (1.0 + jnp.exp(-gate_val)) * (up_sum[rows_at(y), :] * (scale * weight))
        act[rows_at(y), :] = value.astype(jnp.bfloat16)
        return carry

    lax.fori_loop(0, side, activate, 0)

    def produce(s, cols):
        return jnp.dot(act[...], down[:, cols], preferred_element_type=jnp.float32)

    def finish(s, cols, total):
        mixed[:, cols] = hidden[:, cols] + total

    def parts(y, x, core, cols):
        return held.at[y, x, core, :, cols]

    spread, wait_core, wait_spread = reduce_phases(
        here, rows, features, produce, finish, parts, expert_buffers, expert_sems
    )
    run_in_order(((spread, slices, SPREAD_KEYS),))
    with jax.named_scope("drain_spread"):
        wait_core()
        wait_spread()


PROJ_KEYS = ((0.0, 0, 0.0, 0.3), (1.3, 0, 0.0, 0.3), (4.4, 0, 0.0, 0.4), (7.2, 0, 0.0, 0.4))
GATHER_KEYS = ((12.0, 0, 0.0, 1.2), (15.0, 0, 0.0, 1.5), (18.0, 0, 0.0, 1.75), (21.0, 0, 0.0, 1.75))
SPREAD_KEYS = ((0.0, 0, 0.0, 0.45), (1.0, 4, 0.5, 1.75), (5.5, 0, 0.0, 1.75), (9.0, 0, 0.0, 1.75), (14.5, 0, 0.0, 1.75))


def nt_dot(left, right):
    return lax.dot_general(left, right, (((1,), (1,)), ((), ())), preferred_element_type=jnp.float32)


PAD = 16


def run_layer(
    side, depth, lengths, queries, new_keys, new_values, resid, gain, router, named_ids,
    cache_keys, cache_values, out_proj, gate_slab, up_slab, down_slab
):
    rows, width = resid.shape
    n = len(slices_of(width))
    experts = router.shape[0]
    span = cache_keys.shape[1]
    bf, dma = jnp.bfloat16, pltpu.SemaphoreType.DMA
    plane = 2 * side * side
    count = plane * depth
    tail = pl.cdiv(experts + 2, 128) * 128
    vmem, anywhere = pl.BlockSpec(memory_space=pltpu.VMEM), pl.BlockSpec(memory_space=pl.ANY)
    return pl.pallas_call(
        lambda *refs: layer_kernel(side, depth, *refs),
        out_shape=jax.ShapeDtypeStruct((rows, width), jnp.float32),
        in_specs=[pl.BlockSpec(memory_space=pltpu.SMEM)] + [vmem] * 7 + [anywhere] * 6,
        out_specs=vmem,
        scratch_shapes=[
            pltpu.VMEM((rows, span + PAD, KVH * HD), bf),
            pltpu.VMEM((rows, span + PAD, KVH * HD), bf),
            pltpu.VMEM((H // KVH * rows, HD), jnp.float32),
            pltpu.VMEM((H // KVH * rows, HD), jnp.float32),
            pltpu.VMEM((rows, H * HD), bf),
            pltpu.VMEM(out_proj.shape, bf),
            pltpu.VMEM(gate_slab.shape[1:], bf),
            pltpu.VMEM(up_slab.shape[1:], bf),
            pltpu.VMEM(down_slab.shape[1:], bf),
            pltpu.VMEM((plane, rows, H * HD // plane), bf),
            pltpu.VMEM((rows, width), jnp.float32),
            pltpu.VMEM((side, side, 2, depth * rows, width + tail), bf),
            pltpu.VMEM((count * rows, gate_slab.shape[2]), bf),
            pltpu.VMEM((count * rows, gate_slab.shape[2]), jnp.float32),
            pltpu.VMEM((count * rows, gate_slab.shape[2]), jnp.float32),
            dma((2, KVH)),
            dma((4,)),
            dma((2,)),
        ]
        + reduce_shapes(side, 1, rows, width)
        + reduce_shapes(side, depth, rows, width)
        + reduce_sems(side, n) * 2
        + [dma((4,)), dma((n,)), dma((n, side * side - 1)), dma((n,))],
        compiler_params=pltpu.CompilerParams(
            collective_id=0, has_side_effects=True, vmem_limit_bytes=VMEM_LIMIT
        ),
    )(
        lengths, queries, new_keys, new_values, resid, gain, router, named_ids,
        cache_keys, cache_values, out_proj, gate_slab, up_slab, down_slab,
    )


def local(
    resid,
    queries,
    new_keys,
    new_values,
    cache_keys,
    cache_values,
    cache_len,
    out_proj,
    norm_gain,
    router,
    expert_ids,
    gate_slab,
    up_slab,
    down_slab,
):
    side = math.isqrt(lax.axis_size("ep") // 2)
    depth = lax.axis_size("dp")
    return run_layer(
        side, depth, cache_len, queries, new_keys, new_values, resid, norm_gain.reshape(1, -1),
        router.T, expert_ids.T, cache_keys, cache_values, out_proj, gate_slab, up_slab, down_slab,
    )


def solution(mesh):
    in_specs = (
        P(("ep", "dp"), None),
        P(("ep", "dp"), None),
        P(("ep", "dp"), None),
        P(("ep", "dp"), None),
        P(("ep", "dp"), None, None),
        P(("ep", "dp"), None, None),
        P(("ep", "dp")),
        P("ep", None),
        P(),
        P(),
        P(("ep", "dp"), None),
        P(("ep", "dp"), None, None),
        P(("ep", "dp"), None, None),
        P(("ep", "dp"), None, None),
    )
    out_specs = P(("ep", "dp"), None)
    return jax.shard_map(local, mesh=mesh, in_specs=in_specs, out_specs=out_specs, check_vma=False)
```

time: 92.6 us -> 79.1 us (0.85)
  Pallas kernels: 81.9 us -> 77.3 us
  matrix products: 4.03 us -> 0 us
  local copies, waits for them, and re-layouts: 5.02 us -> 1.67 us
  other arithmetic: 1.21 us -> 0 us
    pallas_call x1, Pallas kernels: 81.9 us -> 77.3 us  [run_layer(): pl.pallas_call(lambda *refs: layer_kernel(side, depth, *refs), out_shape=...]
    dot_general x3 -> x0, matrix products: 4.03 us -> none  [the longest x1 3.03 us: attend(): jnp.einsum('tgqd,tcgd->tgqc', query_heads, past_keys, preferred_element_t...]
    unnamed x5 -> x1, local copies, waits for them, and re-layouts: 3.55 us -> 1.67 us
where the time goes in v2:
time: 79.1 us; the launch traced here: 79 us
  Pallas kernels  77.3 us (98%)
  local copies, waits for them, and re-layouts  1.67 us (2%)
    pallas_call x1, Pallas kernels, run_layer(): pl.pallas_call(lambda *refs: layer_kernel(side, depth, *refs), out_shape=...  77.3 us
    unnamed x1, local copies, waits for them, and re-layouts  1.67 us

profile of v2, /device:TPU:0, one launch (start us, length us, event | category | flops | bytes accessed | tf_op | source)
XLA Modules:
  0.0 79.0 jit_solution(3896032727340746973)
XLA Ops:
  0.0 77.3 %shard_map.136 = f32[16,4096]{1,0:T(8,128)} custom-call(s32[16]{0:T(128)} %refs_0_.1, bf16[16,8192]{1,0:T(8,128)(2,1)} %refs_1_.1, bf16[16,512]{1,0:T(8,128)(2,1)} %refs_2_.1, bf16[16,512]{1,0:T(8,128)(2,1)} %refs_3_.1, bf16[16,4096]{1,0:T(8,128)(2,1)} %refs_4_.1, f32[1,4096]{1,0:T(1,128)} %bitcast.4, bf16[16,4096]{1,0:T(8,128)(2,1)} %bitcast.3, ...), custom_call_target="tpu_custom_call" | custom-call | tf_op jit(solution)/shard_map/pallas_call | solution.py:553
  77.3 1.7 %copy.16 = f32[16,4096]{1,0:T(8,128)} copy(f32[16,4096]{1,0:T(8,128)} %shard_map.136) | data formatting | bytes 524288

commit v3 on v2

v3 whole, which is shorter than its diff:
```python
import math

import jax
import jax.numpy as jnp
from jax import lax
from jax.experimental import pallas as pl
from jax.experimental.pallas import tpu as pltpu
from jax.sharding import PartitionSpec as P

D = 4096
H = 64
KVH = 4
HD = 128
TOP = 8


MESH = pl.DeviceIdType.MESH
VMEM_LIMIT = 67_000_000


class Place:
    def __init__(self, side, depth):
        self.side, self.depth = side, depth
        ep = lax.axis_index("ep")
        self.ep = ep
        self.core = lax.rem(ep, 2)
        self.x = lax.rem(ep // 2, side)
        self.y = ep // (2 * side)
        self.z = lax.axis_index("dp")

    def at(self, dy=0, dx=0, dz=0, flip=False):
        y, x = self.line(dy, dx)
        z = lax.rem(self.z + dz, self.depth) if dz else self.z
        core = 1 - self.core if flip else self.core
        return ((y * self.side + x) * 2 + core, z)

    def line(self, dy, dx):
        return lax.rem(self.y + dy, self.side), lax.rem(self.x + dx, self.side)


def announce(devices):
    barrier = pltpu.get_barrier_semaphore()
    for device in devices:
        pl.semaphore_signal(barrier, inc=1, device_id=device, device_id_type=MESH)


def gathered(devices):
    pl.semaphore_wait(pltpu.get_barrier_semaphore(), len(devices))


def remote(src, dst, send, recv, device):
    return pltpu.make_async_remote_copy(
        src_ref=src, dst_ref=dst, send_sem=send, recv_sem=recv, device_id=device, device_id_type=MESH
    )


SLICE = 512
STAGES = 8
ORDER = (
    3, 2, 4, 5, 11, 0, 10, 1, 7, 12, 9, 8, 6, 15, 19, 13, 20, 14, 18, 16,
    17, 27, 23, 28, 21, 22, 25, 24, 26, 30, 29, 36, 31, 32, 35, 33, 34, 59, 38, 60,
    40, 39, 44, 43, 57, 37, 56, 42, 58, 51, 68, 48, 47, 62, 46, 67, 65, 52, 61, 41,
    54, 55, 63, 45, 64, 50, 53, 70, 49, 75, 66, 89, 76, 95, 69, 94, 73, 71, 90, 83,
    93, 72, 81, 78, 84, 103, 98, 97, 74, 80, 77, 86, 79, 82, 85, 87, 124, 123, 120, 127,
    132, 131, 128, 125, 135, 126, 88, 121, 92, 134, 140, 129, 122, 139, 143, 136, 130, 91, 100, 148,
    142, 133, 106, 147, 137, 151, 101, 144, 102, 105, 138, 96, 99, 150, 108, 141, 145, 110, 146, 149,
    114, 107, 159, 111, 109, 104, 116, 155, 112, 154, 153, 115, 113, 117, 152, 118, 119, 158, 156, 157,
)


def slices_of(width):
    return [(start, SLICE) for start in range(0, width, SLICE)]


def task_order(count):
    if count == STAGES:
        return [(code // STAGES, code % STAGES) for code in ORDER]
    return [(task, s) for task in range(20) for s in range(count)]


def reduce_shapes(side, depth, rows, width):
    bf = jnp.bfloat16
    return [
        pltpu.VMEM((depth, side, side, rows, width), bf),
        pltpu.VMEM((depth, side - 1, side, rows, width), bf),
        pltpu.VMEM((depth, side - 1, rows, width), bf),
    ]


def reduce_sems(side, n):
    dma = pltpu.SemaphoreType.DMA
    return [dma((3,)), dma((n,)), dma((n, side - 1, side)), dma((n, side - 1))]


def wide(value):
    return value.astype(jnp.float32)


def wait_bytes(ref, sem):
    pltpu.make_async_copy(ref, ref, sem).wait()


def reduce_phases(here, group, rows, width, produce, finish, part, buffers, sems):
    in1, in2, in3 = buffers
    sent, sem1, sem2, sem3 = sems
    side = here.side
    cuts = slices_of(width)
    every = slice(None)

    def core_copy(s):
        cols = pl.ds(*cuts[s])
        return remote(
            part(every, every, 1 - here.core, cols),
            in1.at[group, :, :, :, cols],
            sent.at[0],
            sem1.at[s],
            here.at(flip=True),
        )

    def offsets(s, a, b):
        return (a, b) if s % 2 == 0 else (b, a)

    def first_copy(s, ja, kb, sending):
        cols = pl.ds(*cuts[s])
        slot = side - ja - 1
        y, x = here.line(*offsets(s, ja, kb))
        return remote(
            in1.at[group, y, x, :, cols],
            in2.at[group, slot, kb, :, cols],
            sent.at[1],
            sem2.at[s, (side - ja if sending else ja) - 1, kb],
            here.at(*offsets(s, ja, 0)),
        )

    def second_copy(s, kb, sending):
        cols = pl.ds(*cuts[s])
        y, x = here.line(*offsets(s, 0, kb))
        return remote(
            in1.at[group, y, x, :, cols],
            in3.at[group, side - kb - 1, :, cols],
            sent.at[2],
            sem3.at[s, (side - kb if sending else kb) - 1],
            here.at(*offsets(s, 0, kb)),
        )

    def phase0(s):
        cols = pl.ds(*cuts[s])

        def put(value, place):
            value = value.astype(jnp.bfloat16).reshape(-1, side, side, 2, rows, cuts[s][1])
            for core in range(2):
                part(every, every, core, cols, place)[...] = value[:, :, :, core]

        produce(s, cols, put)
        core_copy(s).start()

    def phase1(s):
        cols = pl.ds(*cuts[s])
        core_copy(s).wait_recv()
        for a in list(range(1, side)) + [0]:
            for b in list(range(1, side)) + [0]:
                y, x = here.line(*offsets(s, a, b))
                total = wide(part(y, x, here.core, cols)[...]) + wide(in1[group, y, x, :, cols])
                in1[group, y, x, :, cols] = total.astype(jnp.bfloat16)
                if a:
                    first_copy(s, a, b, True).start()

    def phase2(s):
        cols = pl.ds(*cuts[s])
        for b in list(range(1, side)) + [0]:
            y, x = here.line(*offsets(s, 0, b))
            total = wide(in1[group, y, x, :, cols])
            for a in range(1, side):
                first_copy(s, a, b, False).wait_recv()
                total = total + wide(in2[group, a - 1, b, :, cols])
            in1[group, y, x, :, cols] = total.astype(jnp.bfloat16)
            if b:
                second_copy(s, b, True).start()

    def phase3(s):
        cols = pl.ds(*cuts[s])
        total = wide(in1[group, here.y, here.x, :, cols])
        for b in range(1, side):
            second_copy(s, b, False).wait_recv()
            total = total + wide(in3[group, b - 1, :, cols])
        finish(s, cols, total)

    def wait_core():
        wait_bytes(in1.at[group], sent.at[0])

    def wait_sent():
        wait_bytes(in1.at[group, 0 : side - 1], sent.at[1])
        wait_bytes(in1.at[group, 0, 0 : side - 1], sent.at[2])

    return (phase0, phase1, phase2, phase3), wait_core, wait_sent


def gather_phases(here, held, group, features, sems):
    side = here.side
    sent, lsem, csem = sems
    cuts = slices_of(features)
    cuts[-1] = (cuts[-1][0], held.shape[-1] - cuts[-1][0])

    def line_ref(s, ky, kx, core):
        y, x = here.line(ky, kx)
        return held.at[group, y, x, core, :, pl.ds(*cuts[s])]

    def arrival(s, ky, kx):
        return lsem.at[s, (ky % side) * side + kx % side - 1]

    def core_send(s, ky, kx):
        ref = line_ref(s, ky, kx, here.core)
        remote(ref, ref, sent.at[2], csem.at[s], here.at(flip=True)).start()

    def plane_wait(s, ky, kx):
        wait_bytes(line_ref(s, ky, kx, here.core), arrival(s, ky, kx))

    def turn(s, a, b):
        return (a, b) if s % 2 == 0 else (b, a)

    def own_send(s):
        ref = line_ref(s, 0, 0, here.core)
        for j in range(1, side):
            for jy, jx in (turn(s, j, 0), turn(s, 0, j)):
                remote(ref, ref, sent.at[0], arrival(s, -jy, -jx), here.at(jy, jx)).start()
        core_send(s, 0, 0)

    def forward(s):
        for k in range(1, side):
            plane_wait(s, *turn(s, k, 0))
            ref = line_ref(s, *turn(s, k, 0), here.core)
            for j in range(1, side):
                jy, jx = turn(s, 0, j)
                ky, kx = turn(s, k, 0)
                remote(ref, ref, sent.at[1], arrival(s, ky - jy, kx - jx), here.at(jy, jx)).start()
            core_send(s, *turn(s, k, 0))

    def collect(s):
        for b in range(1, side):
            for a in range(side):
                plane_wait(s, *turn(s, a, b))
                core_send(s, *turn(s, a, b))

    def arrive(s):
        wait_bytes(held.at[group, :, :, 1 - here.core, :, pl.ds(*cuts[s])], csem.at[s])

    def wait_sent():
        wait_bytes(held.at[group, 0 : side - 1, 0:2, 0], sent.at[0])
        wait_bytes(held.at[group, 0 : side - 1, 0 : side - 1, 0], sent.at[1])
        wait_bytes(held.at[group, :, :, 0], sent.at[2])

    return (own_send, forward, collect, arrive), wait_sent


def layer_kernel(
    side, depth, lengths, queries, new_keys, new_values, resid, gain, router, named_ids,
    keys_hbm, values_hbm, proj_hbm, gate_hbm, up_hbm, down_hbm, mixed,
    keys, values, query_rows, blend_rows, attended,
    proj, gate, up, down, regrouped, hidden, held, act, gate_sum, up_sum,
    ksem, wsem, xsem, zsem, zsent, *scratch
):
    here, flat = Place(side, depth), Place(side, 1)
    rows, features = resid.shape
    experts = router.shape[0]
    count = 2 * side * side
    width = attended.shape[1] // count
    span = keys_hbm.shape[1]
    group_size = H // KVH
    pieces = count // KVH
    own_group = here.ep // pieces

    def peer(j):
        return lax.rem(here.ep + j, count)

    peers = [(peer(j), here.z) for j in range(1, count)] + [here.at(0, 0, j) for j in range(1, depth)]
    announce(peers)

    def turn_group(i):
        return lax.rem(own_group + 1 + i, KVH)

    def lanes(g):
        return pl.ds(pl.multiple_of(g * HD, HD), HD)

    def cache_copies(i):
        return [
            pltpu.make_async_copy(
                src.at[:, :, lanes(turn_group(i))], dst.at[:, 0:span, lanes(turn_group(i))], ksem.at[n, i]
            )
            for n, (src, dst) in enumerate(((keys_hbm, keys), (values_hbm, values)))
        ]

    for i in range(KVH):
        for copy in cache_copies(i):
            copy.start()
    loads = [
        pltpu.make_async_copy(src, dst, wsem.at[i])
        for i, (src, dst) in enumerate(
            ((proj_hbm, proj), (gate_hbm.at[0], gate), (up_hbm.at[0], up), (down_hbm.at[0], down))
        )
    ]
    loads[0].start()

    first = lax.broadcasted_iota(jnp.int32, (PAD, KVH * HD), 0) == 0
    for new, cache in ((new_keys, keys), (new_values, values)):
        wide_new = new[...].astype(jnp.float32)
        for token in range(rows):
            own = jnp.where(first, wide_new[token : token + 1, :], 0.0)
            cache[token, span:, :] = own.astype(jnp.bfloat16)

    def piece(index):
        return attended.at[:, pl.ds(pl.multiple_of(index * width, 128), width)]

    def exchange(to, source):
        return remote(piece(to), regrouped.at[source], xsem.at[0], xsem.at[1], (to, here.z))

    def attend(i):
        g = turn_group(i)
        for copy in cache_copies(i):
            copy.wait()
        for h in range(group_size):
            query_rows[h * rows : (h + 1) * rows, :] = wide(queries[:, lanes(g * group_size + h)])
        scores = []
        place = lax.broadcasted_iota(jnp.int32, (group_size, span + PAD), 1)
        for token in range(rows):
            query = query_rows[pl.ds(token, group_size, stride=rows), :]
            score = nt_dot(query.astype(jnp.bfloat16), keys[token, :, lanes(g)])
            kept = (place < lengths[token]) | (place == span)
            scores.append(jnp.where(kept, score * (1.0 / math.sqrt(HD)), -1e30))
        score = jnp.concatenate(scores, axis=0)
        grown = jnp.exp(score - jnp.max(score, axis=1, keepdims=True))
        weights = (grown / jnp.sum(grown, axis=1, keepdims=True)).astype(jnp.bfloat16)
        for token in range(rows):
            blend_rows[pl.ds(token, group_size, stride=rows), :] = jnp.dot(
                weights[token * group_size : (token + 1) * group_size, :],
                values[token, :, lanes(g)],
                preferred_element_type=jnp.float32,
            )
        for h in range(group_size):
            attended[:, lanes(g * group_size + h)] = blend_rows[h * rows : (h + 1) * rows, :].astype(
                jnp.bfloat16
            )

    for i in range(KVH):
        if i == KVH - 1:
            gathered(peers)
            for load in loads[1:]:
                load.start()
            for sent in range(i):
                for k in range(pieces):
                    exchange(turn_group(sent) * pieces + k, here.ep).start()
        attend(i)
    for k in range(1, pieces):
        exchange(own_group * pieces + lax.rem(here.ep + k, pieces), here.ep).start()
    regrouped[here.ep] = attended[:, pl.ds(pl.multiple_of(here.ep * width, 128), width)]

    eye = jnp.where(
        lax.broadcasted_iota(jnp.int32, (rows, rows), 0) == lax.broadcasted_iota(jnp.int32, (rows, rows), 1), 1.0, 0.0
    ).astype(jnp.bfloat16)
    label = lax.broadcasted_iota(jnp.int32, (experts, rows), 0)
    hits = jnp.zeros((experts, rows), jnp.float32)
    for k in range(TOP):
        hits = hits + jnp.where(label == named_ids[k : k + 1, :], 1.0, 0.0)
    named = nt_dot(eye, hits.astype(jnp.bfloat16)) > 0.5

    loads[0].wait()
    with jax.named_scope("exchange_wait"):
        wait_bytes(regrouped.at[0 : count - 1], xsem.at[1])

    def produce_proj(s, cols, put):
        left = regrouped[...].reshape(count * rows, width)
        put(jnp.dot(left, proj[:, cols], preferred_element_type=jnp.float32), None)

    squares, logits = [], []
    slices = len(slices_of(features))
    tail_width = held.shape[-1] - features

    def finish_proj(s, cols, total):
        value = resid[:, cols].astype(jnp.float32) + total
        hidden[:, cols] = value
        scaled = (value * gain[:, cols]).astype(jnp.bfloat16)
        held[0, here.y, here.x, here.core, :, cols] = scaled
        if s < slices - 1:
            launch(s)
        squares.append(jnp.sum(value * value, axis=1, keepdims=True))
        logits.append(nt_dot(scaled, router[:, cols]))
        if s == slices - 1:
            scale = lax.rsqrt(jnp.maximum(sum(squares) / features, 0.25))
            scores = sum(logits) * scale
            peak = jnp.max(jnp.where(named, scores, -jnp.inf), axis=1, keepdims=True)
            grown = jnp.where(named, jnp.exp(jnp.where(named, scores - peak, 0.0)), 0.0)
            probs = grown / jnp.sum(grown, axis=1, keepdims=True)
            high = scale.astype(jnp.bfloat16).astype(jnp.float32)
            lane = lax.broadcasted_iota(jnp.int32, (rows, tail_width), 1)
            tail = jnp.where(lane == experts, high, jnp.where(lane == experts + 1, scale - high, 0.0))
            held[0, here.y, here.x, here.core, :, features:] = tail.astype(jnp.bfloat16)
            held[0, here.y, here.x, here.core, :, features : features + experts] = probs.astype(jnp.bfloat16)
            launch(s)

    near, far = slice(0, 1), slice(1, depth)
    plane_rows = count * rows

    def launch(s):
        start, size = slices_of(features)[s]
        cols = pl.ds(start, size if s < slices - 1 else held.shape[-1] - start)
        for j in range(1, depth):
            remote(
                held.at[0, here.y, here.x, here.core, :, cols],
                held.at[depth - j, here.y, here.x, here.core, :, cols],
                zsent.at[0],
                zsem.at[s],
                here.at(0, 0, j),
            ).start()
        near_gather[0](s)

    def relay(s):
        start, size = slices_of(features)[s]
        cols = pl.ds(start, size if s < slices - 1 else held.shape[-1] - start)
        wait_bytes(held.at[far, here.y, here.x, here.core, :, cols], zsem.at[s])
        far_gather[0](s)

    def over(group, body):
        height = plane_rows * (group.stop - group.start)
        if height <= 512:
            body(group, pl.ds(group.start * plane_rows, height))
            return

        def step(j, carry):
            body(pl.ds(j, 1), pl.ds(pl.multiple_of(j * plane_rows, plane_rows), plane_rows))
            return carry

        lax.fori_loop(group.start, group.stop, step, 0)

    started, done = [], {near: 0, far: 0}

    def consume(group, s):
        if not started:
            loads[1].wait()
            loads[2].wait()
            started.append(s)
        start, size = slices_of(features)[s]
        first = done[group] == 0

        def multiply(place, at):
            left = held[place, :, :, :, :, start : start + size].reshape(-1, size)
            for weight, total in ((gate, gate_sum), (up, up_sum)):
                value = jnp.dot(
                    left, weight[start : start + size, :], preferred_element_type=jnp.float32
                )
                total[at, :] = value if first else total[at, :] + value

        over(group, multiply)
        done[group] += 1
        if done[group] == slices:
            over(group, activate)

    expert = (here.ep * depth + here.z) // 2

    def activate(place, at):
        tail = wide(held[place, :, :, :, :, features:].reshape(-1, tail_width))
        lane = lax.broadcasted_iota(jnp.int32, tail.shape, 1)
        weight = jnp.sum(jnp.where(lane == expert, tail, 0.0), axis=1, keepdims=True)
        scale = jnp.sum(
            jnp.where((lane == experts) | (lane == experts + 1), tail, 0.0), axis=1, keepdims=True
        )
        gate_val = gate_sum[at, :] * scale
        value = gate_val / (1.0 + jnp.exp(-gate_val)) * (up_sum[at, :] * (scale * weight))
        act[at, :] = value.astype(jnp.bfloat16)

    in1, in2, in3, in4 = scratch[3:7]
    proj_buffers, expert_buffers, sems = scratch[:3], scratch[3:6], scratch[7:]
    near_sems, far_sems, near_gather_sems, far_gather_sems = sems[:4], sems[4:8], sems[8:11], sems[11:14]
    fsem, fsent = sems[14:]

    def proj_parts(y, x, core, cols, place=None):
        return in1.at[pl.ds(core, 1), y, x, :, cols]

    def expert_parts(group):
        return lambda y, x, core, cols, place=group: held.at[place, y, x, core, :, cols]

    def produce(group):
        def run(s, cols, put):
            if not waited[group]:
                if group is near:
                    loads[3].wait()
                    wait_reduce()
                    wait_bytes(held.at[far, 0, 0, 0], zsent.at[0])
                (wait_near if group is near else wait_far)()
                waited[group].append(s)

            def multiply(place, at):
                put(jnp.dot(act[at, :], down[:, cols], preferred_element_type=jnp.float32), place)

            over(group, multiply)

        return run

    waited = {near: [], far: []}
    halves = [0] * slices

    def settle(s, cols, total):
        mixed[:, cols] = (mixed if halves[s] else hidden)[:, cols] + total
        halves[s] += 1

    def finish_near(s, cols, total):
        settle(s, cols, total[0])

    def finish_far(s, cols, total):
        in1[far, here.y, here.x, :, cols] = total.astype(jnp.bfloat16)
        for j in range(1, depth):
            remote(
                in1.at[j, here.y, here.x, :, cols],
                in4.at[j - 1, :, cols],
                fsent.at[0],
                fsem.at[s],
                here.at(0, 0, j),
            ).start()

    def finish_layer(s):
        cols = pl.ds(*slices_of(features)[s])
        wait_bytes(in4.at[:, :, cols], fsem.at[s])
        settle(s, cols, sum(wide(in4[j, :, cols]) for j in range(depth - 1)))

    reduced = []

    def finish_first(s, cols, total):
        if not reduced:
            wait_core()
        reduced.append(s)
        finish_proj(s, cols, total[0])

    reduce, wait_core, wait_reduce = reduce_phases(
        flat, near, rows, features, produce_proj, finish_first, proj_parts, proj_buffers, near_sems
    )
    near_gather, wait_near = gather_phases(here, held, near, features, near_gather_sems)
    far_gather, wait_far = gather_phases(here, held, far, features, far_gather_sems)
    near_spread, wait_near_core, wait_near_spread = reduce_phases(
        here, near, rows, features, produce(near), finish_near, expert_parts(near), expert_buffers, near_sems
    )
    far_spread, wait_far_core, wait_far_spread = reduce_phases(
        here, far, rows, features, produce(far), finish_far, expert_parts(far), expert_buffers, far_sems
    )

    def use(arrive, group):
        def run(s):
            arrive(s)
            consume(group, s)

        return run

    tasks = (
        *reduce,
        near_gather[1], near_gather[2], use(near_gather[3], near),
        relay, far_gather[1], far_gather[2], use(far_gather[3], far),
        *near_spread, *far_spread, finish_layer,
    )
    for task, s in task_order(slices):
        with jax.named_scope(f"t{task}_{s}"):
            tasks[task](s)
    wait_near_core()
    wait_near_spread()
    wait_far_core()
    wait_far_spread()
    wait_bytes(in1.at[far, 0, 0], fsent.at[0])
    wait_bytes(regrouped.at[0 : count - 1], xsem.at[0])


def nt_dot(left, right):
    return lax.dot_general(left, right, (((1,), (1,)), ((), ())), preferred_element_type=jnp.float32)


PAD = 16


def run_layer(
    side, depth, lengths, queries, new_keys, new_values, resid, gain, router, named_ids,
    cache_keys, cache_values, out_proj, gate_slab, up_slab, down_slab
):
    rows, width = resid.shape
    n = len(slices_of(width))
    experts = router.shape[0]
    span = cache_keys.shape[1]
    bf, dma = jnp.bfloat16, pltpu.SemaphoreType.DMA
    plane = 2 * side * side
    count = plane * depth
    tail = pl.cdiv(experts + 2, 128) * 128
    vmem, anywhere = pl.BlockSpec(memory_space=pltpu.VMEM), pl.BlockSpec(memory_space=pl.ANY)
    return pl.pallas_call(
        lambda *refs: layer_kernel(side, depth, *refs),
        out_shape=jax.ShapeDtypeStruct((rows, width), jnp.float32),
        in_specs=[pl.BlockSpec(memory_space=pltpu.SMEM)] + [vmem] * 7 + [anywhere] * 6,
        out_specs=vmem,
        scratch_shapes=[
            pltpu.VMEM((rows, span + PAD, KVH * HD), bf),
            pltpu.VMEM((rows, span + PAD, KVH * HD), bf),
            pltpu.VMEM((H // KVH * rows, HD), jnp.float32),
            pltpu.VMEM((H // KVH * rows, HD), jnp.float32),
            pltpu.VMEM((rows, H * HD), bf),
            pltpu.VMEM(out_proj.shape, bf),
            pltpu.VMEM(gate_slab.shape[1:], bf),
            pltpu.VMEM(up_slab.shape[1:], bf),
            pltpu.VMEM(down_slab.shape[1:], bf),
            pltpu.VMEM((plane, rows, H * HD // plane), bf),
            pltpu.VMEM((rows, width), jnp.float32),
            pltpu.VMEM((depth, side, side, 2, rows, width + tail), bf),
            pltpu.VMEM((count * rows, gate_slab.shape[2]), bf),
            pltpu.VMEM((count * rows, gate_slab.shape[2]), jnp.float32),
            pltpu.VMEM((count * rows, gate_slab.shape[2]), jnp.float32),
            dma((2, KVH)),
            dma((4,)),
            dma((2,)),
            dma((n,)),
            dma((1,)),
        ]
        + reduce_shapes(side, 1, rows, width)
        + reduce_shapes(side, depth, rows, width)
        + [pltpu.VMEM((depth - 1, rows, width), bf)]
        + reduce_sems(side, n) * 2
        + [dma((3,)), dma((n, side * side - 1)), dma((n,))] * 2
        + [dma((n,)), dma((1,))],
        compiler_params=pltpu.CompilerParams(
            collective_id=0, has_side_effects=True, vmem_limit_bytes=VMEM_LIMIT
        ),
    )(
        lengths, queries, new_keys, new_values, resid, gain, router, named_ids,
        cache_keys, cache_values, out_proj, gate_slab, up_slab, down_slab,
    )


def local(
    resid,
    queries,
    new_keys,
    new_values,
    cache_keys,
    cache_values,
    cache_len,
    out_proj,
    norm_gain,
    router,
    expert_ids,
    gate_slab,
    up_slab,
    down_slab,
):
    side = math.isqrt(lax.axis_size("ep") // 2)
    depth = lax.axis_size("dp")
    return run_layer(
        side, depth, cache_len, queries, new_keys, new_values, resid, norm_gain.reshape(1, -1),
        router.T, expert_ids.T, cache_keys, cache_values, out_proj, gate_slab, up_slab, down_slab,
    )


def solution(mesh):
    in_specs = (
        P(("ep", "dp"), None),
        P(("ep", "dp"), None),
        P(("ep", "dp"), None),
        P(("ep", "dp"), None),
        P(("ep", "dp"), None, None),
        P(("ep", "dp"), None, None),
        P(("ep", "dp")),
        P("ep", None),
        P(),
        P(),
        P(("ep", "dp"), None),
        P(("ep", "dp"), None, None),
        P(("ep", "dp"), None, None),
        P(("ep", "dp"), None, None),
    )
    out_specs = P(("ep", "dp"), None)
    return jax.shard_map(local, mesh=mesh, in_specs=in_specs, out_specs=out_specs, check_vma=False)
```

time: 79.1 us -> 70.3 us (0.89)
  Pallas kernels: 77.3 us -> 68.5 us
    pallas_call x1, Pallas kernels: 77.3 us -> 68.5 us  [run_layer(): pl.pallas_call(lambda *refs: layer_kernel(side, depth, *refs), out_shape=...]
where the time goes in v3:
time: 70.3 us; the launch traced here: 70.2 us
  Pallas kernels  68.5 us (97%)
  local copies, waits for them, and re-layouts  1.67 us (2%)
    pallas_call x1, Pallas kernels, run_layer(): pl.pallas_call(lambda *refs: layer_kernel(side, depth, *refs), out_shape=...  68.5 us
    unnamed x1, local copies, waits for them, and re-layouts  1.67 us

profile of v3, /device:TPU:0, one launch (start us, length us, event | category | flops | bytes accessed | tf_op | source)
XLA Modules:
  0.0 70.2 jit_solution(5662367578514913703)
XLA Ops:
  0.0 68.5 %shard_map.136 = f32[16,4096]{1,0:T(8,128)} custom-call(s32[16]{0:T(128)} %refs_0_.1, bf16[16,8192]{1,0:T(8,128)(2,1)} %refs_1_.1, bf16[16,512]{1,0:T(8,128)(2,1)} %refs_2_.1, bf16[16,512]{1,0:T(8,128)(2,1)} %refs_3_.1, bf16[16,4096]{1,0:T(8,128)(2,1)} %refs_4_.1, f32[1,4096]{1,0:T(1,128)} %bitcast.4, bf16[16,4096]{1,0:T(8,128)(2,1)} %bitcast.3, ...), custom_call_target="tpu_custom_call" | custom-call | tf_op jit(solution)/shard_map/pallas_call | solution.py:587
  68.5 1.7 %copy.16 = f32[16,4096]{1,0:T(8,128)} copy(f32[16,4096]{1,0:T(8,128)} %shard_map.136) | data formatting | bytes 524288

commit v4 on v3

--- a/solution.py
+++ b/solution.py
@@ -57,14 +57,14 @@
 SLICE = 512
 STAGES = 8
 ORDER = (
-    3, 2, 4, 5, 11, 0, 10, 1, 7, 12, 9, 8, 6, 15, 19, 13, 20, 14, 18, 16,
-    17, 27, 23, 28, 21, 22, 25, 24, 26, 30, 29, 36, 31, 32, 35, 33, 34, 59, 38, 60,
-    40, 39, 44, 43, 57, 37, 56, 42, 58, 51, 68, 48, 47, 62, 46, 67, 65, 52, 61, 41,
-    54, 55, 63, 45, 64, 50, 53, 70, 49, 75, 66, 89, 76, 95, 69, 94, 73, 71, 90, 83,
-    93, 72, 81, 78, 84, 103, 98, 97, 74, 80, 77, 86, 79, 82, 85, 87, 124, 123, 120, 127,
-    132, 131, 128, 125, 135, 126, 88, 121, 92, 134, 140, 129, 122, 139, 143, 136, 130, 91, 100, 148,
-    142, 133, 106, 147, 137, 151, 101, 144, 102, 105, 138, 96, 99, 150, 108, 141, 145, 110, 146, 149,
-    114, 107, 159, 111, 109, 104, 116, 155, 112, 154, 153, 115, 113, 117, 152, 118, 119, 158, 156, 157,
+    2, 5, 3, 10, 1, 4, 11, 6, 7, 13, 0, 12, 8, 14, 9, 15, 26, 29, 28, 24,
+    27, 25, 30, 34, 31, 36, 37, 32, 35, 58, 61, 33, 44, 39, 38, 40, 60, 66, 56, 41,
+    59, 69, 42, 46, 47, 48, 45, 43, 52, 57, 55, 62, 51, 54, 74, 53, 63, 82, 65, 68,
+    64, 50, 49, 88, 77, 67, 95, 92, 70, 93, 89, 71, 90, 85, 76, 101, 91, 73, 75, 98,
+    72, 84, 81, 78, 99, 103, 97, 100, 96, 79, 80, 83, 86, 87, 124, 125, 106, 120, 127, 132,
+    133, 126, 128, 121, 135, 122, 123, 141, 140, 130, 136, 129, 143, 134, 149, 105, 148, 138, 131, 144,
+    137, 109, 107, 151, 142, 94, 146, 139, 145, 111, 150, 102, 115, 147, 108, 110, 117, 152, 104, 116,
+    114, 112, 158, 159, 156, 113, 118, 157, 153, 154, 119, 155,
 )
 
 
@@ -75,7 +75,7 @@
 def task_order(count):
     if count == STAGES:
         return [(code // STAGES, code % STAGES) for code in ORDER]
-    return [(task, s) for task in range(20) for s in range(count)]
+    return [(task, s) for task in range(20) if task != 2 for s in range(count)]
 
 
 def reduce_shapes(side, depth, rows, width):
@@ -195,6 +195,69 @@
     return (phase0, phase1, phase2, phase3), wait_core, wait_sent
 
 
+def direct_phases(here, rows, width, produce, finish, part, buffers, sems):
+    in1, in2 = buffers
+    sent, sem1, sem2 = sems
+    side = here.side
+    cuts = slices_of(width)
+    every = slice(None)
+    lines = [(a, b) for a in range(side) for b in range(side)]
+
+    def core_copy(s):
+        cols = pl.ds(*cuts[s])
+        return remote(
+            part(every, every, 1 - here.core, cols),
+            in1.at[:, :, :, :, cols],
+            sent.at[0],
+            sem1.at[s],
+            here.at(flip=True),
+        )
+
+    def phase0(s):
+        cols = pl.ds(*cuts[s])
+
+        def put(value):
+            value = value.astype(jnp.bfloat16).reshape(1, side, side, 2, rows, cuts[s][1])
+            for core in range(2):
+                part(every, every, core, cols)[...] = value[:, :, :, core]
+
+        produce(s, cols, put)
+        core_copy(s).start()
+
+    def phase1(s):
+        cols = pl.ds(*cuts[s])
+        core_copy(s).wait_recv()
+        for a, b in reversed(lines):
+            y, x = here.line(a, b)
+            total = wide(part(y, x, here.core, cols)[0]) + wide(in1[0, y, x, :, cols])
+            in1[0, y, x, :, cols] = total.astype(jnp.bfloat16)
+            if a or b:
+                slot = (side - a) % side * side + (side - b) % side - 1
+                remote(
+                    in1.at[0, y, x, :, cols],
+                    in2.at[slot, :, cols],
+                    sent.at[1],
+                    sem2.at[s, 0],
+                    here.at(a, b),
+                ).start()
+
+    def phase2(s):
+        cols = pl.ds(*cuts[s])
+        wait_bytes(in2.at[:, :, cols], sem2.at[s, 0])
+        total = wide(in1[0, here.y, here.x, :, cols])
+        for slot in range(side * side - 1):
+            total = total + wide(in2[slot, :, cols])
+        finish(s, cols, total)
+
+    def wait_core():
+        wait_bytes(in1, sent.at[0])
+
+    def wait_sent():
+        wait_bytes(in2, sent.at[1])
+
+    return (phase0, phase1, phase2), wait_core, wait_sent
+
+
 def gather_phases(here, held, group, features, sems):
     side = here.side
     sent, lsem, csem = sems
@@ -253,9 +316,9 @@
 
 
 def layer_kernel(
-    side, depth, lengths, queries, new_keys, new_values, resid, gain, router, named_ids,
+    side, depth, lengths, queries_hbm, new_keys_hbm, new_values_hbm, resid_hbm, gain_hbm, router_hbm, ids_hbm,
     keys_hbm, values_hbm, proj_hbm, gate_hbm, up_hbm, down_hbm, mixed,
-    keys, values, query_rows, blend_rows, attended,
+    queries, new_keys, new_values, resid, gain, router, named_ids, isem, keys, values, query_rows, blend_rows, attended,
     proj, gate, up, down, regrouped, hidden, held, act, gate_sum, up_sum,
     ksem, wsem, xsem, zsem, zsent, *scratch
 ):
@@ -274,6 +337,17 @@
 
     peers = [(peer(j), here.z) for j in range(1, count)] + [here.at(0, 0, j) for j in range(1, depth)]
     announce(peers)
+    inputs = [
+        pltpu.make_async_copy(src, dst, isem.at[i])
+        for i, (src, dst) in enumerate(
+            (
+                (queries_hbm, queries), (new_keys_hbm, new_keys), (new_values_hbm, new_values),
+                (resid_hbm, resid), (gain_hbm, gain), (router_hbm, router), (ids_hbm, named_ids),
+            )
+        )
+    ]
+    for copy in inputs[:3]:
+        copy.start()
 
     def turn_group(i):
         return lax.rem(own_group + 1 + i, KVH)
@@ -298,9 +372,13 @@
             ((proj_hbm, proj), (gate_hbm.at[0], gate), (up_hbm.at[0], up), (down_hbm.at[0], down))
         )
     ]
+    for copy in inputs[3:]:
+        copy.start()
     loads[0].start()
 
     first = lax.broadcasted_iota(jnp.int32, (PAD, KVH * HD), 0) == 0
+    for copy in inputs[:3]:
+        copy.wait()
     for new, cache in ((new_keys, keys), (new_values, values)):
         wide_new = new[...].astype(jnp.float32)
         for token in range(rows):
@@ -353,6 +431,8 @@
         exchange(own_group * pieces + lax.rem(here.ep + k, pieces), here.ep).start()
     regrouped[here.ep] = attended[:, pl.ds(pl.multiple_of(here.ep * width, 128), width)]
 
+    for copy in inputs[3:]:
+        copy.wait()
     eye = jnp.where(
         lax.broadcasted_iota(jnp.int32, (rows, rows), 0) == lax.broadcasted_iota(jnp.int32, (rows, rows), 1), 1.0, 0.0
     ).astype(jnp.bfloat16)
@@ -368,7 +448,7 @@
 
     def produce_proj(s, cols, put):
         left = regrouped[...].reshape(count * rows, width)
-        put(jnp.dot(left, proj[:, cols], preferred_element_type=jnp.float32), None)
+        put(jnp.dot(left, proj[:, cols], preferred_element_type=jnp.float32))
 
     squares, logits = [], []
     slices = len(slices_of(features))
@@ -466,12 +546,12 @@
         value = gate_val / (1.0 + jnp.exp(-gate_val)) * (up_sum[at, :] * (scale * weight))
         act[at, :] = value.astype(jnp.bfloat16)
 
-    in1, in2, in3, in4 = scratch[3:7]
-    proj_buffers, expert_buffers, sems = scratch[:3], scratch[3:6], scratch[7:]
+    in1, in2, in3, in4 = scratch[2:6]
+    proj_buffers, expert_buffers, sems = scratch[:2], scratch[2:5], scratch[6:]
     near_sems, far_sems, near_gather_sems, far_gather_sems = sems[:4], sems[4:8], sems[8:11], sems[11:14]
     fsem, fsent = sems[14:]
 
-    def proj_parts(y, x, core, cols, place=None):
+    def proj_parts(y, x, core, cols):
         return in1.at[pl.ds(core, 1), y, x, :, cols]
 
     def expert_parts(group):
@@ -526,10 +606,11 @@
         if not reduced:
             wait_core()
         reduced.append(s)
-        finish_proj(s, cols, total[0])
-
-    reduce, wait_core, wait_reduce = reduce_phases(
-        flat, near, rows, features, produce_proj, finish_first, proj_parts, proj_buffers, near_sems
+        finish_proj(s, cols, total)
+
+    reduce, wait_core, wait_reduce = direct_phases(
+        flat, rows, features, produce_proj, finish_first, proj_parts, proj_buffers,
+        (near_sems[0], near_sems[1], near_sems[3]),
     )
     near_gather, wait_near = gather_phases(here, held, near, features, near_gather_sems)
     far_gather, wait_far = gather_phases(here, held, far, features, far_gather_sems)
@@ -548,7 +629,7 @@
         return run
 
     tasks = (
-        *reduce,
+        reduce[0], reduce[1], None, reduce[2],
         near_gather[1], near_gather[2], use(near_gather[3], near),
         relay, far_gather[1], far_gather[2], use(far_gather[3], far),
         *near_spread, *far_spread, finish_layer,
@@ -587,9 +668,14 @@
     return pl.pallas_call(
         lambda *refs: layer_kernel(side, depth, *refs),
         out_shape=jax.ShapeDtypeStruct((rows, width), jnp.float32),
-        in_specs=[pl.BlockSpec(memory_space=pltpu.SMEM)] + [vmem] * 7 + [anywhere] * 6,
+        in_specs=[pl.BlockSpec(memory_space=pltpu.SMEM)] + [anywhere] * 13,
         out_specs=vmem,
         scratch_shapes=[
+            pltpu.VMEM(array.shape, array.dtype)
+            for array in (queries, new_keys, new_values, resid, gain, router, named_ids)
+        ]
+        + [
+            dma((7,)),
             pltpu.VMEM((rows, span + PAD, KVH * HD), bf),
             pltpu.VMEM((rows, span + PAD, KVH * HD), bf),
             pltpu.VMEM((H // KVH * rows, HD), jnp.float32),
@@ -611,7 +697,10 @@
             dma((n,)),
             dma((1,)),
         ]
-        + reduce_shapes(side, 1, rows, width)
+        + [
+            pltpu.VMEM((1, side, side, rows, width), bf),
+            pltpu.VMEM((side * side - 1, rows, width), bf),
+        ]
         + reduce_shapes(side, depth, rows, width)
         + [pltpu.VMEM((depth - 1, rows, width), bf)]
         + reduce_sems(side, n) * 2

time: 70.3 us -> 68.7 us (0.977)
  Pallas kernels: 68.5 us -> 66.8 us
    pallas_call x1, Pallas kernels: 68.5 us -> 66.8 us  [run_layer(): pl.pallas_call(lambda *refs: layer_kernel(side, depth, *refs), out_shape=...]
where the time goes in v4:
time: 68.7 us; the launch traced here: 68.5 us
  Pallas kernels  66.8 us (97%)
  local copies, waits for them, and re-layouts  1.67 us (2%)
    pallas_call x1, Pallas kernels, run_layer(): pl.pallas_call(lambda *refs: layer_kernel(side, depth, *refs), out_shape=...  66.8 us
    unnamed x1, local copies, waits for them, and re-layouts  1.67 us

profile of v4, /device:TPU:0, one launch (start us, length us, event | category | flops | bytes accessed | tf_op | source)
XLA Modules:
  0.0 68.5 jit_solution(11574027375855771861)
XLA Ops:
  0.0 66.8 %shard_map.136 = f32[16,4096]{1,0:T(8,128)} custom-call(s32[16]{0:T(128)} %refs_0_.1, bf16[16,8192]{1,0:T(8,128)(2,1)} %refs_1_.1, bf16[16,512]{1,0:T(8,128)(2,1)} %refs_2_.1, bf16[16,512]{1,0:T(8,128)(2,1)} %refs_3_.1, bf16[16,4096]{1,0:T(8,128)(2,1)} %refs_4_.1, f32[1,4096]{1,0:T(1,128)} %bitcast.4, bf16[16,4096]{1,0:T(8,128)(2,1)} %bitcast.3, ...), custom_call_target="tpu_custom_call" | custom-call | tf_op jit(solution)/shard_map/pallas_call | solution.py:668
  66.8 1.7 %copy.16 = f32[16,4096]{1,0:T(8,128)} copy(f32[16,4096]{1,0:T(8,128)} %shard_map.136) | data formatting | bytes 524288
